TPU v7x, 256 devices: a whole 4x4x8 slice. The times are simulated.
256 devices in a mesh: seq: 64 (over z, y, x_hi), head: 4 (over x_lo, core).
Axes of the slice: x: 4 (x_hi: 2, x_lo: 2; x = x_hi * 2 + x_lo), y: 4, z: 8, core: 2. Of those that a mesh axis runs over, the one named last changes fastest.
Arguments:
- queries: bfloat16 [8192, 4096], P('seq', 'head'), may hold values from -12 to 12
- keys: bfloat16 [8192, 2048], P('seq', 'head'), may hold values from -12 to 12
- values: bfloat16 [8192, 2048], P('seq', 'head'), may hold values from -6 to 6
- block_order: int32 [128], replicated, may hold values from 0 to 127, each once
Outputs:
- attn: bfloat16 [8192, 4096], P(('seq', 'head'))
- lse: float32 [16, 8192], P('head', 'seq')
Inputs may be any that keep to these rules, and one draw needn't show every extreme that they name: device-order block j (rows j * 64 to j * 64 + 63) holds sequence positions block_order[j] * 64 onward, in order.
All inputs are finite; a program needn't handle non-finite values.
Results may differ from a plain program's by a relative error of at most 0.006.
Values may be sent and summed in bfloat16 or wider, within the bound.
A program may use at most 128 MiB of HBM per device.

v0:
```python
import math

import jax
import jax.numpy as jnp
from jax import lax
from jax.sharding import PartitionSpec as P

HEAD_SIZE = 256
QUERY_GROUP = 2


def side_by_side(arrays, axis, dim, along):
    ends, at = ([], 0)
    for a in arrays[:-1]:
        at += a.shape[along]
        ends.append(at)
    both = jnp.concatenate(arrays, axis=along)
    return tuple(jnp.split(lax.all_gather(both, axis, axis=dim, tiled=True), ends, axis=along))


def positions(order, first_block, count, blk):
    ids = lax.dynamic_slice_in_dim(order, first_block, count, 0)
    return (ids[:, None] * blk + jnp.arange(blk, dtype=jnp.int32)[None, :]).reshape(-1)


def row_positions(order, start, length, blk):
    index = start + jnp.arange(length, dtype=jnp.int32)
    return order[index // blk] * blk + index % blk


def attend(state, queries, keys, values, query_pos, key_pos, scale):
    maximum, total, accum = state
    scores = jnp.einsum("qhgd,khd->hgqk", queries, keys, preferred_element_type=jnp.float32) * scale
    allowed = key_pos[None, :] <= query_pos[:, None]
    scores = jnp.where(allowed, scores, -1e30)
    fresh = jnp.maximum(maximum, jnp.max(scores, axis=-1))
    weights = jnp.where(allowed, jnp.exp(scores - fresh[..., None]), 0.0)
    factor = jnp.exp(maximum - fresh)
    total = total * factor + jnp.sum(weights, axis=-1)
    update = jnp.einsum(
        "hgqk,khd->qhgd", weights.astype(jnp.bfloat16), values, preferred_element_type=jnp.float32
    )
    accum = accum * jnp.transpose(factor, (2, 0, 1))[..., None] + update
    return (fresh, total, accum)


def local(queries, keys, values, block_order):
    rows = queries.shape[0]
    blk = rows // 2
    head_dim = HEAD_SIZE
    group = QUERY_GROUP
    kv_local = keys.shape[1] // head_dim
    scale = head_dim ** (-0.5)
    my_index = lax.axis_index("seq")
    query_head_count = queries.reshape(rows, kv_local, group, head_dim)
    query_pos = positions(block_order, my_index * 2, 2, blk)

    def absorb(state, part_keys, part_values, key_pos, first, count):
        key_rows = part_keys.shape[0]
        sub_state = (state[0], state[1], state[2])
        key_heads = part_keys.reshape(key_rows, count, head_dim)
        value_heads = part_values.reshape(key_rows, count, head_dim)
        sub_state = attend(
            sub_state, query_head_count, key_heads, value_heads, query_pos, key_pos, scale
        )
        return (
            state[0].at[first : first + count].set(sub_state[0]),
            state[1].at[first : first + count].set(sub_state[1]),
            state[2].at[:, first : first + count].set(sub_state[2]),
        )

    initial = (
        jnp.full((kv_local, group, rows), -1e30, jnp.float32),
        jnp.zeros((kv_local, group, rows), jnp.float32),
        jnp.zeros((rows, kv_local, group, head_dim), jnp.float32),
    )
    piece_keys, piece_values = side_by_side((keys, values), "seq", 0, 1)
    length = piece_keys.shape[0]
    block_rows = math.gcd(length, 2048)
    count = length // block_rows

    def inner(index, inner_state):
        offset = (index * block_rows).astype(jnp.int32)
        block_keys = lax.dynamic_slice_in_dim(piece_keys, offset, block_rows, 0)
        block_values = lax.dynamic_slice_in_dim(piece_values, offset, block_rows, 0)
        key_pos = row_positions(block_order, offset, block_rows, blk)
        return absorb(inner_state, block_keys, block_values, key_pos, 0, kv_local)

    state = lax.fori_loop(0, count, inner, initial)
    maximum, total, accum = state
    output = accum / jnp.transpose(total, (2, 0, 1))[..., None]
    output = output.reshape(rows, kv_local * group * head_dim).astype(jnp.bfloat16)
    lse = (maximum + jnp.log(total)).reshape(kv_local * group, rows)
    attn = lax.all_to_all(output, "head", split_axis=0, concat_axis=1, tiled=True)
    return (attn, lse)


def solution(mesh):
    in_specs = (P("seq", "head"), P("seq", "head"), P("seq", "head"), P())
    out_specs = (P(("seq", "head"), None), P("head", "seq"))
    return jax.shard_map(local, mesh=mesh, in_specs=in_specs, out_specs=out_specs, check_vma=False)
```

profile of v0, /device:TPU:1, one launch (start us, length us, event | category | flops | bytes accessed | tf_op | source)
XLA Modules:
  0.0 406.3 jit_solution(2367149622278398409)
XLA Ops:
  10.1 1.1 copy.22
  12.1 258.9 %all-gather.2.cloned.1.call-done = bf16[8192,1024]{0,1:T(8,128)(2,1)} async-done(((bf16[128,1024]{0,1:T(8,128)(2,1)}), bf16[8192,1024]{0,1:T(8,128)(2,1)}) %all-gather.2.cloned.1.call-update) | async-done | bytes 16777232 | tf_op jit(solution)/shard_map/all_gather | solution.py:18
  271.0 11.6 %fusion.29 = (bf16[8192,512]{0,1:T(8,128)(2,1)}, bf16[8192,512]{0,1:T(8,128)(2,1)}) fusion(bf16[8192,1024]{0,1:T(8,128)(2,1)} %all-gather.2.cloned.1.call-done), kind=kLoop, calls=%fused_computation.47 | loop fusion | bytes 33554432 | tf_op jit(solution)/shard_map/split | solution.py:18
  282.5 102.7 %while.47 = (s32[]{:T(128)}, f32[2,2,128]{2,1,0:T(2,128)S(1)}, f32[2,2,128]{2,1,0:T(2,128)S(1)}, f32[128,2,2,256]{0,3,2,1:T(8,128)S(1)}, s32[128]{0:T(128)S(1)},...) while((s32[]{:T(128)}, f32[2,2,128]{2,1,0:T(2,128)S(1)}, ...), condition=%wide.region_3.4_spmd.clone, body=%wide.region_0.3_spmd.clone.sunk | while | flops 1088102528 | bytes 44415204 | solution.py:89
  282.5 4.0 constant_dynamic-slice_fusion.3
  286.6 12.6 %gather_fusion = s32[2048]{0:T(1024)S(1)} fusion(s32[128]{0:T(128)S(1)} %get-tuple-element.509, s32[2048]{0:T(1024)S(1)} %broadcast_clamp_fusion.2), kind=kCustom, calls=%fused_computation.clone.clone.1 | custom fusion | bytes 24576 | tf_op jit(solution)/shard_map/while/body/eval_jaxpr/gather | solution.py:28
  299.7 3.1 fusion.49
  302.9 4.2 %fusion.54 = f32[128,2,2,256]{0,3,2,1:T(8,128)S(1)} fusion(bf16[2048,2,256,1]{0,2,3,1:T(8,128)(2,1)} %bitcast.68, f32[2,2048,128,2]{2,1,3,0:T(8,128)} %get-tuple-element.477, f32[2,2,128]{2,1,0:T(2,128)S(1)} %fusion.50, pred[128,2048]{0,1:T(8,128)(4,1)S(1)} %broadcast_compare_fusion.2, f32[128,2,2,256]{0,3,2,1:T(8,128)S(1)} %get-tuple-element.495, ...), kind=kOutput, calls=%fused_computation.14.clone.1 | convolution fusion | flops 542507008 | bytes 7606273 | tf_op jit(solution)/shard_map/while/body/eval_jaxpr/hgqk,khd->qhgd/dot_general | solution.py:40
  307.1 1.0 fusion.51
  308.2 4.0 constant_dynamic-slice_fusion.3
  312.3 12.6 %gather_fusion = s32[2048]{0:T(1024)S(1)} fusion(s32[128]{0:T(128)S(1)} %get-tuple-element.509, s32[2048]{0:T(1024)S(1)} %broadcast_clamp_fusion.2), kind=kCustom, calls=%fused_computation.clone.clone.1 | custom fusion | bytes 24576 | tf_op jit(solution)/shard_map/while/body/eval_jaxpr/gather | solution.py:28
  325.4 3.1 fusion.49
  328.5 4.2 %fusion.54 = f32[128,2,2,256]{0,3,2,1:T(8,128)S(1)} fusion(bf16[2048,2,256,1]{0,2,3,1:T(8,128)(2,1)} %bitcast.68, f32[2,2048,128,2]{2,1,3,0:T(8,128)} %get-tuple-element.477, f32[2,2,128]{2,1,0:T(2,128)S(1)} %fusion.50, pred[128,2048]{0,1:T(8,128)(4,1)S(1)} %broadcast_compare_fusion.2, f32[128,2,2,256]{0,3,2,1:T(8,128)S(1)} %get-tuple-element.495, ...), kind=kOutput, calls=%fused_computation.14.clone.1 | convolution fusion | flops 542507008 | bytes 7606273 | tf_op jit(solution)/shard_map/while/body/eval_jaxpr/hgqk,khd->qhgd/dot_general | solution.py:40
  332.8 1.0 fusion.51
  333.9 4.0 constant_dynamic-slice_fusion.3
  338.0 12.6 %gather_fusion = s32[2048]{0:T(1024)S(1)} fusion(s32[128]{0:T(128)S(1)} %get-tuple-element.509, s32[2048]{0:T(1024)S(1)} %broadcast_clamp_fusion.2), kind=kCustom, calls=%fused_computation.clone.clone.1 | custom fusion | bytes 24576 | tf_op jit(solution)/shard_map/while/body/eval_jaxpr/gather | solution.py:28
  351.1 3.1 fusion.49
  354.2 4.2 %fusion.54 = f32[128,2,2,256]{0,3,2,1:T(8,128)S(1)} fusion(bf16[2048,2,256,1]{0,2,3,1:T(8,128)(2,1)} %bitcast.68, f32[2,2048,128,2]{2,1,3,0:T(8,128)} %get-tuple-element.477, f32[2,2,128]{2,1,0:T(2,128)S(1)} %fusion.50, pred[128,2048]{0,1:T(8,128)(4,1)S(1)} %broadcast_compare_fusion.2, f32[128,2,2,256]{0,3,2,1:T(8,128)S(1)} %get-tuple-element.495, ...), kind=kOutput, calls=%fused_computation.14.clone.1 | convolution fusion | flops 542507008 | bytes 7606273 | tf_op jit(solution)/shard_map/while/body/eval_jaxpr/hgqk,khd->qhgd/dot_general | solution.py:40
  359.6 4.0 constant_dynamic-slice_fusion.3
  363.6 12.6 %gather_fusion = s32[2048]{0:T(1024)S(1)} fusion(s32[128]{0:T(128)S(1)} %get-tuple-element.509, s32[2048]{0:T(1024)S(1)} %broadcast_clamp_fusion.2), kind=kCustom, calls=%fused_computation.clone.clone.1 | custom fusion | bytes 24576 | tf_op jit(solution)/shard_map/while/body/eval_jaxpr/gather | solution.py:28
  376.8 3.1 fusion.49
  379.9 4.2 %fusion.54 = f32[128,2,2,256]{0,3,2,1:T(8,128)S(1)} fusion(bf16[2048,2,256,1]{0,2,3,1:T(8,128)(2,1)} %bitcast.68, f32[2,2048,128,2]{2,1,3,0:T(8,128)} %get-tuple-element.477, f32[2,2,128]{2,1,0:T(2,128)S(1)} %fusion.50, pred[128,2048]{0,1:T(8,128)(4,1)S(1)} %broadcast_compare_fusion.2, f32[128,2,2,256]{0,3,2,1:T(8,128)S(1)} %get-tuple-element.495, ...), kind=kOutput, calls=%fused_computation.14.clone.1 | convolution fusion | flops 542507008 | bytes 7606273 | tf_op jit(solution)/shard_map/while/body/eval_jaxpr/hgqk,khd->qhgd/dot_general | solution.py:40
  386.4 7.3 %all-to-all-start = ((bf16[4,32,1024]{2,1,0:T(8,128)(2,1)}), bf16[4,32,1024]{2,1,0:T(8,128)(2,1)S(1)}, u32[]{:S(2)}, u32[]{:S(2)}) async-start(bf16[4,32,1024]{2,1,0:T(8,128)(2,1)} %convert_element_type.18), calls=%async_computation | async-start | bytes 524288 | tf_op jit(solution)/shard_map/all_to_all | solution.py:94
  394.3 4.5 %all-to-all-done = bf16[4,32,1024]{2,1,0:T(8,128)(2,1)S(1)} async-done(((bf16[4,32,1024]{2,1,0:T(8,128)(2,1)}), bf16[4,32,1024]{2,1,0:T(8,128)(2,1)S(1)}, u32[]{:S(2)}, u32[]{:S(2)}) %all-to-all-start) | async-done | bytes 262176 | tf_op jit(solution)/shard_map/all_to_all | solution.py:94
  (67 shorter events, 10.6 us)
Async XLA Ops:
  7.2 263.8 %all-gather.2.cloned.1.call-start = ((), (), s32[]{:S(2)}) async-start(), calls=%async_computation.1 | async-start | bytes 17039360 | tf_op jit(solution)/shard_map/all_gather | solution.py:18
  12.1 270.5 %copy-start = (s32[128]{0:T(128)S(1)}, s32[128]{0:T(128)}, u32[]{:S(2)}) copy-start(s32[128]{0:T(128)} %param.21) | copy-start | bytes 1540
  302.8 4.3 %copy-start.1 = (f32[2,2048,128,2]{2,1,3,0:T(8,128)S(1)}, f32[2,2048,128,2]{2,1,3,0:T(8,128)}, u32[]{:S(2)}) copy-start(f32[2,2048,128,2]{2,1,3,0:T(8,128)} %get-tuple-element.477) | copy-start | bytes 12582916 | tf_op jit(solution)/shard_map/while
  328.5 4.3 %copy-start.1 = (f32[2,2048,128,2]{2,1,3,0:T(8,128)S(1)}, f32[2,2048,128,2]{2,1,3,0:T(8,128)}, u32[]{:S(2)}) copy-start(f32[2,2048,128,2]{2,1,3,0:T(8,128)} %get-tuple-element.477) | copy-start | bytes 12582916 | tf_op jit(solution)/shard_map/while
  354.2 4.3 %copy-start.1 = (f32[2,2048,128,2]{2,1,3,0:T(8,128)S(1)}, f32[2,2048,128,2]{2,1,3,0:T(8,128)}, u32[]{:S(2)}) copy-start(f32[2,2048,128,2]{2,1,3,0:T(8,128)} %get-tuple-element.477) | copy-start | bytes 12582916 | tf_op jit(solution)/shard_map/while
  379.9 4.3 %copy-start.1 = (f32[2,2048,128,2]{2,1,3,0:T(8,128)S(1)}, f32[2,2048,128,2]{2,1,3,0:T(8,128)}, u32[]{:S(2)}) copy-start(f32[2,2048,128,2]{2,1,3,0:T(8,128)} %get-tuple-element.477) | copy-start | bytes 12582916 | tf_op jit(solution)/shard_map/while
  386.4 12.4 %all-to-all-start = ((bf16[4,32,1024]{2,1,0:T(8,128)(2,1)}), bf16[4,32,1024]{2,1,0:T(8,128)(2,1)S(1)}, u32[]{:S(2)}, u32[]{:S(2)}) async-start(bf16[4,32,1024]{2,1,0:T(8,128)(2,1)} %convert_element_type.18), calls=%async_computation | async-start | bytes 524288 | tf_op jit(solution)/shard_map/all_to_all | solution.py:94
Sparse Core Ops, SparseCore 0:
  12.0 258.9 all-gather.1
where the time goes:
time: 407 us; the launch traced here: 406 us
  waiting for transfers between devices  263 us (65%)
  local copies, waits for them, and re-layouts  83.5 us (21%)
  matrix products  29.3 us (7%)
  between operations  14.1 us (3%)
  other arithmetic  8.32 us (2%)
  starting transfers between devices  7.35 us (2%)
    all_gather x1, waiting for transfers between devices, side_by_side(): lax.all_gather(both, axis, axis=dim, tiled=True)  259 us
    gather x4, local copies, waits for them, and re-layouts, row_positions(): return order[index // blk] * blk + index % blk  50.5 us
    dot_general x4, matrix products, attend(): jnp.einsum('hgqk,khd->qhgd', weights.astype(jnp.bfloat16), values, prefer...  17 us
    dynamic_slice x4, local copies, waits for them, and re-layouts, inner(): block_values = lax.dynamic_slice_in_dim(piece_values, offset, block_rows, 0)  16 us
    dot_general x4, matrix products, attend(): jnp.einsum('qhgd,khd->hgqk', queries, keys, preferred_element_type=jnp.fl...  12.3 us
    split x1, local copies, waits for them, and re-layouts, side_by_side(): jnp.split(lax.all_gather(both, axis, axis=dim, tiled=True), ends, axis=al...  11.6 us
  transfers between devices with their start and end apart: 2, of which 2 were waited for; matrix products, arithmetic and copies ran while one was open for 1% of the time, Pallas kernels for 0%

commit v1 on v0

v1 whole, which is shorter than its diff:
```python
import functools

import jax
import jax.numpy as jnp
from jax import lax
from jax.experimental import pallas as pl
from jax.experimental.pallas import tpu as pltpu
from jax.sharding import PartitionSpec as P

MESH = pl.DeviceIdType.MESH
HEAD = 256
ROWS = 128
BLK = 64
NZ, NY = 8, 4
NEG = -1e30
FLOOR = -1e6
LOG2E = 1.4426950408889634
LN2 = 0.6931471805599453
F32 = jnp.float32
BF16 = jnp.bfloat16

RIGHT_SLOTS = (0, 1, 2, 3, 7)
LEFT_SLOTS = (0, 4, 5, 6, 7)
SLOT_DZ = (0, -1, -2, -3, 1, 2, 3, 4)
QUERY_DY = (0, -1, 1, 2)


def combine(parts):
    top = functools.reduce(jnp.maximum, [lse for _, lse in parts])
    weights = [jnp.exp2(lse - top) for _, lse in parts]
    total = functools.reduce(jnp.add, weights)
    scale = 1.0 / total
    out = functools.reduce(jnp.add, [o.astype(F32) * (w * scale) for (o, _), w in zip(parts, weights)])
    return out, top + jnp.log2(total)


def kernel(q_ref, k_ref, v_ref, order_ref, attn_ref, lse_ref,
           qbuf, kbuf, vbuf, vm, vsw, qpos, acc, mx, ls,
           osend, lsend, orecv, lrecv, obuf, abuf, lxs, lxr,
           local_sem, send_sem, recv_sem):
    s = lax.axis_index("seq")
    g = lax.axis_index("head")
    z = s // (2 * NY)
    y = (s // 2) % NY
    c = s % 2

    def at(dz, dy):
        return (((z + dz + NZ) % NZ) * NY + (y + dy + NY) % NY) * 2 + c

    partner = (s + 1 - 2 * c, g)
    up, down = (at(1, 0), g), (at(-1, 0), g)
    fore, back = (at(0, 1), g), (at(0, -1), g)

    loads = [
        pltpu.make_async_copy(v_ref, vm, local_sem.at[0]),
        pltpu.make_async_copy(k_ref.at[:, pl.ds(pl.multiple_of(c * HEAD, HEAD), HEAD)], kbuf.at[0, pl.ds(0, ROWS), :], local_sem.at[1]),
    ]
    for hd in range(2):
        loads.append(pltpu.make_async_copy(
            q_ref.at[:, pl.ds(pl.multiple_of(c * 2 * HEAD + hd * HEAD, HEAD), HEAD)],
            qbuf.at[0, pl.ds(hd * ROWS, ROWS), :], local_sem.at[2 + hd]))
    for copy in loads:
        copy.start()

    line = []
    for r in range(2):
        for e in range(4):
            if r or e:
                line.append(((s if r == 0 else s + 1 - 2 * c), (g + e) % 4))
    barrier = pltpu.get_barrier_semaphore()
    for peer in line + [up, down, fore, back]:
        pl.semaphore_signal(barrier, inc=1, device_id=peer, device_id_type=MESH)

    table = {}

    def message(name, src, dst, device):
        i = len(table)
        table[name] = pltpu.make_async_remote_copy(
            src_ref=src, dst_ref=dst, send_sem=send_sem.at[i], recv_sem=recv_sem.at[i],
            device_id=device, device_id_type=MESH)

    other = 1 - c
    for hd in range(2):
        message(("xq", hd), q_ref.at[:, pl.ds(pl.multiple_of(other * 2 * HEAD + hd * HEAD, HEAD), HEAD)],
                qbuf.at[1, pl.ds(hd * ROWS, ROWS), :], partner)
    message("xk", k_ref.at[:, pl.ds(pl.multiple_of(other * HEAD, HEAD), HEAD)], kbuf.at[0, pl.ds(ROWS, ROWS), :], partner)
    message("xv", vsw, vbuf.at[0, :, pl.ds(ROWS, ROWS)], partner)
    for h in range(2):
        def kpart(slot):
            return kbuf.at[slot, pl.ds(h * ROWS, ROWS), :]

        def vpart(slot):
            return vbuf.at[slot, :, pl.ds(h * ROWS, ROWS)]

        for t in range(1, 5):
            message(("rk", h, t), kpart(RIGHT_SLOTS[t - 1]), kpart(RIGHT_SLOTS[t]), up)
            message(("lv", h, t), vpart(LEFT_SLOTS[t - 1]), vpart(LEFT_SLOTS[t]), down)
            if t < 4:
                message(("lk", h, t), kpart(LEFT_SLOTS[t - 1]), kpart(LEFT_SLOTS[t]), down)
                message(("rv", h, t), vpart(RIGHT_SLOTS[t - 1]), vpart(RIGHT_SLOTS[t]), up)

        def qpart(slot, hd):
            return qbuf.at[slot * 2 + h, pl.ds(hd * ROWS, ROWS), :]

        for hd in range(2):
            message(("qr", h, hd), qpart(0, hd), qpart(1, hd), fore)
            message(("ql", h, hd), qpart(0, hd), qpart(2, hd), back)
        message(("qrr", h), qpart(1, 0), qpart(3, 0), fore)
        message(("qll", h), qpart(2, 1), qpart(3, 1), back)
    for n in range(6):
        device = fore if n % 2 == 0 else back
        message(("o", n), osend.at[n], orecv.at[n], device)
        message(("l", n), lsend.at[n], lrecv.at[n], device)
    message("lx", lxs, lxr, partner)

    def line_copy(r, e, index, sender_c, sender_g, device):
        rows = pl.ds(pl.multiple_of(((sender_g + e) % 4) * 32, 32), 32)
        cols = pl.ds(pl.multiple_of((2 * sender_g + sender_c) * 2 * HEAD, 2 * HEAD), 2 * HEAD)
        return pltpu.make_async_remote_copy(
            src_ref=obuf.at[r, rows, :], dst_ref=abuf.at[:, cols],
            send_sem=send_sem.at[index], recv_sem=recv_sem.at[index], device_id=device, device_id_type=MESH)

    base = len(table)
    line_out, line_in = {}, {}
    for r in range(2):
        for e in range(4):
            if r or e:
                index = base + r * 4 + e
                there = s if r == 0 else s + 1 - 2 * c
                line_out[r, e] = line_copy(r, e, index, c, g, (there, (g + e) % 4))
                line_in[r, e] = line_copy(r, e, index, c if r == 0 else other, (g + 4 - e) % 4, (there, (g + e) % 4))

    started = []

    def send(name):
        table[name].start()
        started.append(table[name])

    def arrive(name):
        table[name].wait_recv()

    loads[0].wait()

    def flipped(column):
        v = vm[:, pl.ds(pl.multiple_of(column * HEAD, HEAD), HEAD)]
        return v.astype(F32).T.astype(BF16)

    vbuf[0, :, 0:ROWS] = flipped(c)
    vsw[...] = flipped(other)

    lane = lax.broadcasted_iota(jnp.int32, (8, HEAD), 1)
    for slot in range(4):
        for h in range(2):
            origin = (z * NY + (y + QUERY_DY[slot] + NY) % NY) * 2 + (c if h == 0 else other)
            first, second = order_ref[2 * origin] * BLK, order_ref[2 * origin + 1] * BLK
            inside = lane % ROWS
            qpos[slot * 2 + h] = jnp.where(inside < BLK, first + inside, second + inside - BLK)

    def key_bases(slot):
        out = []
        for h in range(2):
            origin = (((z + SLOT_DZ[slot] + NZ) % NZ) * NY + y) * 2 + (c if h == 0 else other)
            out += [order_ref[2 * origin] * BLK, order_ref[2 * origin + 1] * BLK]
        return out

    iota = lax.broadcasted_iota(jnp.int32, (BLK, HEAD), 0)

    def step(i, slots, bases, first):
        q = qbuf[i]
        position = qpos[i, 0:1, :]
        scores = []
        for slot, base4 in zip(slots, bases):
            raw = lax.dot_general(kbuf[slot], q, (((1,), (1,)), ((), ())), preferred_element_type=F32)
            parts = [
                jnp.where(iota <= position - base4[b], raw[b * BLK:(b + 1) * BLK] * (LOG2E / 16.0), NEG)
                for b in range(4)
            ]
            scores.append(jnp.concatenate(parts, axis=0))
        best = functools.reduce(jnp.maximum, [jnp.max(t.reshape(32, 8, HEAD), axis=0) for t in scores])
        best = jnp.max(best, axis=0, keepdims=True)
        old = jnp.full((1, HEAD), FLOOR, F32) if first else mx[i, 0:1, :]
        fresh = jnp.maximum(old, best)
        weights = [jnp.exp2(t - fresh) for t in scores]
        sums = functools.reduce(jnp.add, [jnp.sum(w.reshape(32, 8, HEAD), axis=0) for w in weights])
        update = functools.reduce(jnp.add, [
            lax.dot_general(vbuf[slot], w.astype(BF16), (((1,), (0,)), ((), ())), preferred_element_type=F32)
            for slot, w in zip(slots, weights)
        ])
        if first:
            return update, fresh, sums
        factor = jnp.exp2(old - fresh)
        return acc[i] * factor + update, fresh, ls[i] * factor + sums

    def attend(tiles, slots, first=False):
        bases = [key_bases(slot) for slot in slots]
        start, stop = tiles

        def body(j, carry):
            for i in (start + 2 * j, start + 2 * j + 1):
                a, m, l = step(i, slots, bases, first)
                acc[i] = a
                mx[i] = jnp.broadcast_to(m, (8, HEAD))
                ls[i] = l
            return carry

        lax.fori_loop(0, (stop - start) // 2, body, 0)

    def finish(i, slots, bases):
        a, m, l8 = step(i, slots, bases, False)
        l = jnp.sum(l8, axis=0, keepdims=True)
        some = l > 0.0
        inverse = jnp.where(some, 1.0 / jnp.where(some, l, 1.0), 0.0)
        return a * inverse, jnp.where(some, m + jnp.log2(jnp.where(some, l, 1.0)), NEG)

    for copy in loads[1:]:
        copy.wait()
    pl.semaphore_wait(barrier, 11)

    send(("rk", 0, 1))
    send(("lk", 0, 1))
    send(("xq", 0))
    send(("xq", 1))
    for hd in range(2):
        send(("qr", 0, hd))
        send(("ql", 0, hd))
    send(("rv", 0, 1))
    send(("lv", 0, 1))
    send("xk")
    send("xv")

    def ring(h, t):
        arrive(("rk", h, t))
        if t < 4:
            send(("rk", h, t + 1))
            arrive(("lk", h, t))
            if t < 3:
                send(("lk", h, t + 1))
            arrive(("rv", h, t))
            if t < 3:
                send(("rv", h, t + 1))
        arrive(("lv", h, t))
        if t < 4:
            send(("lv", h, t + 1))

    def spread(h):
        for hd in range(2):
            send(("qr", h, hd))
            send(("ql", h, hd))

    def relay(h):
        arrive(("qr", h, 0))
        send(("qrr", h))
        arrive(("ql", h, 1))
        send(("qll", h))
        arrive(("qr", h, 1))
        arrive(("ql", h, 0))

    def relayed(h):
        arrive(("qrr", h))
        arrive(("qll", h))

    relay(0)
    ring(0, 1)
    arrive(("xq", 0))
    arrive(("xq", 1))
    spread(1)
    arrive("xk")
    send(("rk", 1, 1))
    send(("lk", 1, 1))
    ring(0, 2)
    arrive("xv")
    send(("rv", 1, 1))
    send(("lv", 1, 1))
    relayed(0)
    relay(1)
    attend((0, 2), (0,), first=True)
    ring(1, 1)
    ring(0, 3)
    attend((2, 6), (0,), first=True)
    attend((0, 6), (1, 4))
    ring(1, 2)
    ring(0, 4)
    relayed(1)
    attend((6, 8), (0,), first=True)
    attend((6, 8), (1, 4))
    attend((0, 8), (2, 5))
    ring(1, 3)
    attend((0, 8), (3, 6))
    ring(1, 4)

    bases = [key_bases(7)]

    def post(n, o, lse):
        osend[n] = o.astype(BF16)
        lsend[n] = jnp.broadcast_to(lse, (8, HEAD))
        send(("o", n))
        send(("l", n))

    def taken(n):
        arrive(("o", n))
        arrive(("l", n))
        return orecv[n], lrecv[n, 0:1, :]

    post(0, *finish(6, (7,), bases))
    post(1, *finish(7, (7,), bases))
    post(2, *finish(5, (7,), bases))
    post(3, *finish(2, (7,), bases))
    mine = finish(4, (7,), bases)
    post(4, *combine([mine, taken(0)]))
    mine = finish(3, (7,), bases)
    post(5, *combine([mine, taken(1)]))

    def result(r, pieces):
        out, lse = combine(pieces)
        flat = out.T.astype(BF16)
        for hd in range(2):
            obuf[r, :, hd * HEAD:(hd + 1) * HEAD] = flat[hd * ROWS:(hd + 1) * ROWS]
        for e in range(4):
            if r or e:
                line_out[r, e].start()
                started.append(line_out[r, e])
        return lse * LN2

    own = [finish(0, (7,), bases), finish(1, (7,), bases)]
    lse0 = result(0, [own[0], taken(3), taken(4)])
    for hd in range(2):
        lse_ref[pl.ds(2 * c + hd, 1), :] = lse0[:, hd * ROWS:(hd + 1) * ROWS]
    lse1 = result(1, [own[1], taken(2), taken(5)])
    lxs[...] = jnp.concatenate(
        [jnp.broadcast_to(lse1[:, 0:ROWS], (4, ROWS)), jnp.broadcast_to(lse1[:, ROWS:], (4, ROWS))], axis=0)
    send("lx")
    cols = pl.ds(pl.multiple_of((2 * g + c) * 2 * HEAD, 2 * HEAD), 2 * HEAD)
    abuf[:, cols] = obuf[0, pl.ds(pl.multiple_of(g * 32, 32), 32), :]
    arrive("lx")
    for hd in range(2):
        lse_ref[pl.ds(2 * other + hd, 1), :] = lxr[4 * hd:4 * hd + 1, :]
    for copy in line_in.values():
        copy.wait_recv()
    attn_ref[...] = abuf[...]
    for copy in started:
        copy.wait_send()


def local(queries, keys, values, block_order):
    any_space = pl.BlockSpec(memory_space=pl.ANY)
    vmem = pl.BlockSpec(memory_space=pltpu.VMEM)
    return pl.pallas_call(
        kernel,
        out_shape=(
            jax.ShapeDtypeStruct((32, 4096), BF16),
            jax.ShapeDtypeStruct((4, ROWS), F32),
        ),
        in_specs=[any_space, any_space, any_space, pl.BlockSpec(memory_space=pltpu.SMEM)],
        out_specs=(vmem, vmem),
        scratch_shapes=[
            pltpu.VMEM((8, 256, HEAD), BF16),
            pltpu.VMEM((8, 256, HEAD), BF16),
            pltpu.VMEM((8, HEAD, 256), BF16),
            pltpu.VMEM((ROWS, 2 * HEAD), BF16),
            pltpu.VMEM((HEAD, ROWS), BF16),
            pltpu.VMEM((8, 8, HEAD), jnp.int32),
            pltpu.VMEM((8, HEAD, 256), F32),
            pltpu.VMEM((8, 8, 256), F32),
            pltpu.VMEM((8, 8, 256), F32),
            pltpu.VMEM((6, HEAD, 256), BF16),
            pltpu.VMEM((6, 8, 256), F32),
            pltpu.VMEM((6, HEAD, 256), BF16),
            pltpu.VMEM((6, 8, 256), F32),
            pltpu.VMEM((2, ROWS, 2 * HEAD), BF16),
            pltpu.VMEM((32, 4096), BF16),
            pltpu.VMEM((8, ROWS), F32),
            pltpu.VMEM((8, ROWS), F32),
            pltpu.SemaphoreType.DMA((4,)),
            pltpu.SemaphoreType.DMA((72,)),
            pltpu.SemaphoreType.DMA((72,)),
        ],
        compiler_params=pltpu.CompilerParams(collective_id=0, has_side_effects=True, vmem_limit_bytes=60 * 1024 * 1024),
        name="attention",
    )(queries, keys, values, block_order)


def solution(mesh):
    in_specs = (P("seq", "head"), P("seq", "head"), P("seq", "head"), P())
    out_specs = (P(("seq", "head"), None), P("head", "seq"))
    return jax.shard_map(local, mesh=mesh, in_specs=in_specs, out_specs=out_specs, check_vma=False)
```

time: 407 us -> 59.9 us (0.15)
  waiting for transfers between devices: 263 us -> 0 us
  local copies, waits for them, and re-layouts: 83.5 us -> 2.25 us
  Pallas kernels: 0 us -> 56.8 us
  matrix products: 29.3 us -> 0 us
  between operations: 14.1 us -> 0.65 us
  other arithmetic: 8.32 us -> 0 us
  starting transfers between devices: 7.35 us -> 0 us
    all_gather x1 -> x0, waiting for transfers between devices: 259 us -> none  [side_by_side(): lax.all_gather(both, axis, axis=dim, tiled=True)]
    pallas_call x0 -> x1, Pallas kernels: none -> 56.8 us  [local(): pl.pallas_call(kernel, out_shape=(jax.ShapeDtypeStruct((32, 4096), BF16),...]
    gather x4 -> x0, local copies, waits for them, and re-layouts: 50.5 us -> none  [row_positions(): return order[index // blk] * blk + index % blk]
    dot_general x8 -> x0, matrix products: 29.3 us -> none  [the longest x4 17 us: attend(): jnp.einsum('hgqk,khd->qhgd', weights.astype(jnp.bfloat16), values, prefer...]
    dynamic_slice x4 -> x0, local copies, waits for them, and re-layouts: 16 us -> none  [inner(): block_values = lax.dynamic_slice_in_dim(piece_values, offset, block_rows, 0)]
    split x1 -> x0, local copies, waits for them, and re-layouts: 11.6 us -> none  [side_by_side(): jnp.split(lax.all_gather(both, axis, axis=dim, tiled=True), ends, axis=al...]
    all_to_all x1 -> x0, starting transfers between devices: 7.31 us -> none  [local(): lax.all_to_all(output, 'head', split_axis=0, concat_axis=1, tiled=True)]
    all_to_all x1 -> x0, waiting for transfers between devices: 4.45 us -> none  [local(): lax.all_to_all(output, 'head', split_axis=0, concat_axis=1, tiled=True)]
  transfers between devices with their start and end apart: 2 -> 0, of which waited for: 2 -> 0; matrix products, arithmetic and copies ran while one was open for 1% -> 0% of each run, Pallas kernels for 0% -> 0%
where the time goes in v1:
time: 59.9 us; the launch traced here: 59.7 us
  Pallas kernels  56.8 us (95%)
  local copies, waits for them, and re-layouts  2.25 us (4%)
  between operations  0.65 us (1%)
    pallas_call x1, Pallas kernels, local(): pl.pallas_call(kernel, out_shape=(jax.ShapeDtypeStruct((32, 4096), BF16),...  56.8 us
    unnamed x4, local copies, waits for them, and re-layouts  2.25 us

profile of v1, /device:TPU:1, one launch (start us, length us, event | category | flops | bytes accessed | tf_op | source)
XLA Modules:
  0.0 59.7 jit_solution(16138771566221737562)
XLA Ops:
  0.6 56.8 %attention.1 = (bf16[32,4096]{1,0:T(8,128)(2,1)}, f32[4,128]{1,0:T(4,128)}) custom-call(bf16[128,1024]{1,0:T(8,128)(2,1)} %q_ref.1, bf16[128,512]{1,0:T(8,128)(2,1)} %k_ref.1, bf16[128,512]{1,0:T(8,128)(2,1)} %v_ref.1, s32[128]{0:T(128)} %order_ref.1), custom_call_target="tpu_custom_call" | custom-call | tf_op jit(solution)/shard_map/attention/pallas_call | solution.py:347
  57.5 0.0 copy-start
  57.5 1.7 %copy.8 = bf16[32,4096]{1,0:T(8,128)(2,1)} copy(bf16[32,4096]{1,0:T(8,128)(2,1)} %get-tuple-element.4) | data formatting | bytes 524288
  59.2 0.0 copy-done
  59.2 0.6 copy.9
Async XLA Ops:
  57.5 1.7 %copy-start = (f32[4,128]{1,0:T(4,128)S(1)}, f32[4,128]{1,0:T(4,128)}, u32[]{:S(2)}) copy-start(f32[4,128]{1,0:T(4,128)} %get-tuple-element.5) | copy-start | bytes 6148

commit v2 on v1

--- a/solution.py
+++ b/solution.py
@@ -13,8 +13,9 @@
 BLK = 64
 NZ, NY = 8, 4
 NEG = -1e30
+BIG = 1e30
+SCALE = 1.4426950408889634 / 16.0
 FLOOR = -1e6
-LOG2E = 1.4426950408889634
 LN2 = 0.6931471805599453
 F32 = jnp.float32
 BF16 = jnp.bfloat16
@@ -36,7 +37,7 @@
 
 def kernel(q_ref, k_ref, v_ref, order_ref, attn_ref, lse_ref,
            qbuf, kbuf, vbuf, vm, vsw, qpos, acc, mx, ls,
-           osend, lsend, orecv, lrecv, obuf, abuf, lxs, lxr,
+           osend, lsend, orecv, lrecv, obuf, abuf, lxs, lxr, sa, sb, pa, pb, km, qm,
            local_sem, send_sem, recv_sem):
     s = lax.axis_index("seq")
     g = lax.axis_index("head")
@@ -59,6 +60,10 @@
         loads.append(pltpu.make_async_copy(
             q_ref.at[:, pl.ds(pl.multiple_of(c * 2 * HEAD + hd * HEAD, HEAD), HEAD)],
             qbuf.at[0, pl.ds(hd * ROWS, ROWS), :], local_sem.at[2 + hd]))
+    loads += [
+        pltpu.make_async_copy(k_ref.at[:, pl.ds(pl.multiple_of((1 - c) * HEAD, HEAD), HEAD)], km, local_sem.at[4]),
+        pltpu.make_async_copy(q_ref.at[:, pl.ds(pl.multiple_of((1 - c) * 2 * HEAD, HEAD), 2 * HEAD)], qm, local_sem.at[5]),
+    ]
     for copy in loads:
         copy.start()
 
@@ -81,9 +86,9 @@
 
     other = 1 - c
     for hd in range(2):
-        message(("xq", hd), q_ref.at[:, pl.ds(pl.multiple_of(other * 2 * HEAD + hd * HEAD, HEAD), HEAD)],
-                qbuf.at[1, pl.ds(hd * ROWS, ROWS), :], partner)
-    message("xk", k_ref.at[:, pl.ds(pl.multiple_of(other * HEAD, HEAD), HEAD)], kbuf.at[0, pl.ds(ROWS, ROWS), :], partner)
+        message(("xq", hd), qm.at[:, pl.ds(hd * HEAD, HEAD)],
+                qbuf.at[4, pl.ds(hd * ROWS, ROWS), :], partner)
+    message("xk", km, kbuf.at[0, pl.ds(ROWS, ROWS), :], partner)
     message("xv", vsw, vbuf.at[0, :, pl.ds(ROWS, ROWS)], partner)
     for h in range(2):
         def kpart(slot):
@@ -100,7 +105,7 @@
                 message(("rv", h, t), vpart(RIGHT_SLOTS[t - 1]), vpart(RIGHT_SLOTS[t]), up)
 
         def qpart(slot, hd):
-            return qbuf.at[slot * 2 + h, pl.ds(hd * ROWS, ROWS), :]
+            return qbuf.at[h * 4 + slot, pl.ds(hd * ROWS, ROWS), :]
 
         for hd in range(2):
             message(("qr", h, hd), qpart(0, hd), qpart(1, hd), fore)
@@ -154,7 +159,7 @@
             origin = (z * NY + (y + QUERY_DY[slot] + NY) % NY) * 2 + (c if h == 0 else other)
             first, second = order_ref[2 * origin] * BLK, order_ref[2 * origin + 1] * BLK
             inside = lane % ROWS
-            qpos[slot * 2 + h] = jnp.where(inside < BLK, first + inside, second + inside - BLK)
+            qpos[h * 4 + slot] = jnp.where(inside < BLK, first + inside, second + inside - BLK)
 
     def key_bases(slot):
         out = []
@@ -165,52 +170,95 @@
 
     iota = lax.broadcasted_iota(jnp.int32, (BLK, HEAD), 0)
 
-    def step(i, slots, bases, first):
+    score_buffers, weight_buffers = (sa, sb), (pa, pb)
+    bases_of = {}
+    queue = []
+    count = [0]
+
+    def stage_scores(item):
+        i, slots = item["tile"], item["slots"]
+        into = score_buffers[item["turn"] % 2]
         q = qbuf[i]
+        for n, slot in enumerate(slots):
+            into[n * 256:(n + 1) * 256, :] = lax.dot_general(
+                kbuf[slot], q, (((1,), (1,)), ((), ())), preferred_element_type=F32)
+
+    def stage_weights(item):
+        i, slots = item["tile"], item["slots"]
+        source, into = score_buffers[item["turn"] % 2], weight_buffers[item["turn"] % 2]
+        diagonal = slots == (0,) and i in (0, 4)
+        first = slots == (0,)
         position = qpos[i, 0:1, :]
-        scores = []
-        for slot, base4 in zip(slots, bases):
-            raw = lax.dot_general(kbuf[slot], q, (((1,), (1,)), ((), ())), preferred_element_type=F32)
-            parts = [
-                jnp.where(iota <= position - base4[b], raw[b * BLK:(b + 1) * BLK] * (LOG2E / 16.0), NEG)
-                for b in range(4)
-            ]
-            scores.append(jnp.concatenate(parts, axis=0))
-        best = functools.reduce(jnp.maximum, [jnp.max(t.reshape(32, 8, HEAD), axis=0) for t in scores])
-        best = jnp.max(best, axis=0, keepdims=True)
+        for slot in slots:
+            if slot not in bases_of:
+                bases_of[slot] = key_bases(slot)
+        bases = [base for slot in slots for base in bases_of[slot]]
+
+        def raw(b):
+            block = source[b * BLK:(b + 1) * BLK, :]
+            return jnp.where(iota <= position - bases[b], block, NEG) if diagonal else block
+
         old = jnp.full((1, HEAD), FLOOR, F32) if first else mx[i, 0:1, :]
+        allowed = [base <= position for base in bases]
+        best = functools.reduce(jnp.maximum, [
+            jnp.where(allowed[b], jnp.max(raw(b).reshape(8, 8, HEAD), axis=0), NEG) for b in range(len(bases))])
+        best = jnp.max(best, axis=0, keepdims=True) * SCALE
         fresh = jnp.maximum(old, best)
-        weights = [jnp.exp2(t - fresh) for t in scores]
-        sums = functools.reduce(jnp.add, [jnp.sum(w.reshape(32, 8, HEAD), axis=0) for w in weights])
+        sums = None
+        for b in range(len(bases)):
+            weights = jnp.exp2(raw(b) * SCALE - jnp.where(allowed[b], fresh, BIG))
+            part = jnp.sum(weights.reshape(8, 8, HEAD), axis=0)
+            sums = part if sums is None else sums + part
+            into[b * BLK:(b + 1) * BLK, :] = weights.astype(BF16)
+        if first:
+            item["factor"] = None
+        else:
+            item["factor"] = jnp.exp2(old - fresh)
+            sums = ls[i] * item["factor"] + sums
+        if item["last"]:
+            item["top"], item["sums"] = fresh, sums
+        else:
+            mx[i] = jnp.broadcast_to(fresh, (8, HEAD))
+            ls[i] = sums
+
+    def stage_values(item):
+        i, slots = item["tile"], item["slots"]
+        source = weight_buffers[item["turn"] % 2]
         update = functools.reduce(jnp.add, [
-            lax.dot_general(vbuf[slot], w.astype(BF16), (((1,), (0,)), ((), ())), preferred_element_type=F32)
-            for slot, w in zip(slots, weights)
+            lax.dot_general(vbuf[slot], source[n * 256:(n + 1) * 256, :], (((1,), (0,)), ((), ())), preferred_element_type=F32)
+            for n, slot in enumerate(slots)
         ])
-        if first:
-            return update, fresh, sums
-        factor = jnp.exp2(old - fresh)
-        return acc[i] * factor + update, fresh, ls[i] * factor + sums
-
-    def attend(tiles, slots, first=False):
-        bases = [key_bases(slot) for slot in slots]
-        start, stop = tiles
-
-        def body(j, carry):
-            for i in (start + 2 * j, start + 2 * j + 1):
-                a, m, l = step(i, slots, bases, first)
-                acc[i] = a
-                mx[i] = jnp.broadcast_to(m, (8, HEAD))
-                ls[i] = l
-            return carry
-
-        lax.fori_loop(0, (stop - start) // 2, body, 0)
-
-    def finish(i, slots, bases):
-        a, m, l8 = step(i, slots, bases, False)
-        l = jnp.sum(l8, axis=0, keepdims=True)
-        some = l > 0.0
-        inverse = jnp.where(some, 1.0 / jnp.where(some, l, 1.0), 0.0)
-        return a * inverse, jnp.where(some, m + jnp.log2(jnp.where(some, l, 1.0)), NEG)
+        if item["factor"] is not None:
+            update = acc[i] * item["factor"] + update
+        if item["last"]:
+            l = jnp.sum(item["sums"], axis=0, keepdims=True)
+            some = l > 0.0
+            inverse = jnp.where(some, 1.0 / jnp.where(some, l, 1.0), 0.0)
+            item["done"](update * inverse, jnp.where(some, item["top"] + jnp.log2(jnp.where(some, l, 1.0)), NEG))
+        else:
+            acc[i] = update
+
+    def advance():
+        if queue and queue[-1]["stage"] == 0:
+            stage_scores(queue[-1])
+        for item in queue[::-1]:
+            if item["stage"] == 1:
+                stage_weights(item)
+            elif item["stage"] == 2:
+                stage_values(item)
+        for item in queue:
+            item["stage"] += 1
+        queue[:] = [item for item in queue if item["stage"] < 3]
+
+    def push(tiles, slots, done=None):
+        for i in tiles:
+            queue.append({"tile": i, "slots": slots, "turn": count[0], "stage": 0, "last": done is not None, "done": done})
+            count[0] += 1
+            advance()
+
+    def flush():
+        while queue:
+            advance()
 
     for copy in loads[1:]:
         copy.wait()
@@ -218,77 +266,102 @@
 
     send(("rk", 0, 1))
     send(("lk", 0, 1))
-    send(("xq", 0))
-    send(("xq", 1))
+    send("xk")
+    send("xv")
     for hd in range(2):
         send(("qr", 0, hd))
         send(("ql", 0, hd))
     send(("rv", 0, 1))
     send(("lv", 0, 1))
-    send("xk")
-    send("xv")
-
-    def ring(h, t):
+    send(("xq", 0))
+    send(("xq", 1))
+
+    def ring_keys(h, t):
         arrive(("rk", h, t))
         if t < 4:
             send(("rk", h, t + 1))
             arrive(("lk", h, t))
             if t < 3:
                 send(("lk", h, t + 1))
+
+    def ring_values(h, t):
+        arrive(("lv", h, t))
+        if t < 4:
+            send(("lv", h, t + 1))
             arrive(("rv", h, t))
             if t < 3:
                 send(("rv", h, t + 1))
-        arrive(("lv", h, t))
-        if t < 4:
-            send(("lv", h, t + 1))
-
-    def spread(h):
-        for hd in range(2):
-            send(("qr", h, hd))
-            send(("ql", h, hd))
-
-    def relay(h):
-        arrive(("qr", h, 0))
-        send(("qrr", h))
-        arrive(("ql", h, 1))
-        send(("qll", h))
-        arrive(("qr", h, 1))
-        arrive(("ql", h, 0))
+
+    def ring(h, t):
+        ring_keys(h, t)
+        ring_values(h, t)
+
+    def spread(hd):
+        arrive(("xq", hd))
+        send(("qr", 1, hd))
+        send(("ql", 1, hd))
+
+    def relay(h, part):
+        if part == 0:
+            arrive(("qr", h, 0))
+            send(("qrr", h))
+            arrive(("ql", h, 0))
+        else:
+            arrive(("ql", h, 1))
+            send(("qll", h))
+            arrive(("qr", h, 1))
 
     def relayed(h):
         arrive(("qrr", h))
         arrive(("qll", h))
 
-    relay(0)
-    ring(0, 1)
-    arrive(("xq", 0))
-    arrive(("xq", 1))
+    def cross_values():
+        arrive("xv")
+        send(("rv", 1, 1))
+        send(("lv", 1, 1))
+
+    def cross_keys():
+        arrive("xk")
+        send(("rk", 1, 1))
+        send(("lk", 1, 1))
+
+    ring_keys(0, 1)
+    cross_keys()
+    relay(0, 0)
+    relay(0, 1)
+    ring_values(0, 1)
+    cross_values()
+    push((0, 1, 2), (0,))
+    spread(0)
     spread(1)
-    arrive("xk")
-    send(("rk", 1, 1))
-    send(("lk", 1, 1))
-    ring(0, 2)
-    arrive("xv")
-    send(("rv", 1, 1))
-    send(("lv", 1, 1))
+    ring_keys(0, 2)
     relayed(0)
-    relay(1)
-    attend((0, 2), (0,), first=True)
-    ring(1, 1)
-    ring(0, 3)
-    attend((2, 6), (0,), first=True)
-    attend((0, 6), (1, 4))
-    ring(1, 2)
+    push((3,), (0,))
+    ring_keys(1, 1)
+    push((4,), (0,))
+    ring_values(0, 2)
+    relay(1, 0)
+    relay(1, 1)
+    push((5, 6), (0,))
+    ring_values(1, 1)
+    push((0, 1, 2, 3), (1, 4))
+    ring_keys(0, 3)
+    relayed(1)
+    push((4, 5), (1, 4))
+    ring_keys(1, 2)
+    push((6,), (1, 4))
+    push((7,), (0,))
+    ring_values(0, 3)
+    push((7,), (1, 4))
+    ring_values(1, 2)
+    push((0, 1, 2, 3), (2, 5))
     ring(0, 4)
-    relayed(1)
-    attend((6, 8), (0,), first=True)
-    attend((6, 8), (1, 4))
-    attend((0, 8), (2, 5))
-    ring(1, 3)
-    attend((0, 8), (3, 6))
+    push((4, 5), (2, 5))
+    ring_keys(1, 3)
+    push((6, 7), (2, 5))
+    ring_values(1, 3)
+    push((0, 1, 2, 3, 4, 5, 6, 7), (3, 6))
     ring(1, 4)
-
-    bases = [key_bases(7)]
 
     def post(n, o, lse):
         osend[n] = o.astype(BF16)
@@ -301,14 +374,23 @@
         arrive(("l", n))
         return orecv[n], lrecv[n, 0:1, :]
 
-    post(0, *finish(6, (7,), bases))
-    post(1, *finish(7, (7,), bases))
-    post(2, *finish(5, (7,), bases))
-    post(3, *finish(2, (7,), bases))
-    mine = finish(4, (7,), bases)
-    post(4, *combine([mine, taken(0)]))
-    mine = finish(3, (7,), bases)
-    post(5, *combine([mine, taken(1)]))
+    own = {}
+
+    def done_with(tile):
+        def done(o, lse):
+            if tile in direct:
+                post(direct[tile], o, lse)
+            elif tile in (2, 5):
+                n = 0 if tile == 2 else 1
+                post(4 + n, *combine([(o, lse), taken(n)]))
+            else:
+                own[tile] = (o, lse)
+        return done
+
+    direct = {3: 0, 7: 1, 6: 2, 1: 3}
+    for tile in (3, 7, 6, 1, 0, 4, 2, 5):
+        push((tile,), (7,), done_with(tile))
+    flush()
 
     def result(r, pieces):
         out, lse = combine(pieces)
@@ -321,11 +403,10 @@
                 started.append(line_out[r, e])
         return lse * LN2
 
-    own = [finish(0, (7,), bases), finish(1, (7,), bases)]
     lse0 = result(0, [own[0], taken(3), taken(4)])
     for hd in range(2):
         lse_ref[pl.ds(2 * c + hd, 1), :] = lse0[:, hd * ROWS:(hd + 1) * ROWS]
-    lse1 = result(1, [own[1], taken(2), taken(5)])
+    lse1 = result(1, [own[4], taken(2), taken(5)])
     lxs[...] = jnp.concatenate(
         [jnp.broadcast_to(lse1[:, 0:ROWS], (4, ROWS)), jnp.broadcast_to(lse1[:, ROWS:], (4, ROWS))], axis=0)
     send("lx")
@@ -342,7 +423,7 @@
 
 
 def local(queries, keys, values, block_order):
-    any_space = pl.BlockSpec(memory_space=pl.ANY)
+    any_space = pl.BlockSpec(memory_space=pltpu.HBM)
     vmem = pl.BlockSpec(memory_space=pltpu.VMEM)
     return pl.pallas_call(
         kernel,
@@ -370,13 +451,19 @@
             pltpu.VMEM((32, 4096), BF16),
             pltpu.VMEM((8, ROWS), F32),
             pltpu.VMEM((8, ROWS), F32),
-            pltpu.SemaphoreType.DMA((4,)),
+            pltpu.VMEM((512, HEAD), F32),
+            pltpu.VMEM((512, HEAD), F32),
+            pltpu.VMEM((512, HEAD), BF16),
+            pltpu.VMEM((512, HEAD), BF16),
+            pltpu.VMEM((ROWS, HEAD), BF16),
+            pltpu.VMEM((ROWS, 2 * HEAD), BF16),
+            pltpu.SemaphoreType.DMA((6,)),
             pltpu.SemaphoreType.DMA((72,)),
             pltpu.SemaphoreType.DMA((72,)),
         ],
-        compiler_params=pltpu.CompilerParams(collective_id=0, has_side_effects=True, vmem_limit_bytes=60 * 1024 * 1024),
+        compiler_params=pltpu.CompilerParams(collective_id=0, has_side_effects=True, vmem_limit_bytes=24 * 1024 * 1024),
         name="attention",
-    )(queries, keys, values, block_order)
+    )(*[pltpu.with_memory_space_constraint(a, pltpu.HBM) for a in (queries, keys, values, block_order)])
 
 
 def solution(mesh):

time: 59.9 us -> 53.7 us (0.90)
  Pallas kernels: 56.8 us -> 51.7 us
  local copies, waits for them, and re-layouts: 2.25 us -> 1.28 us
    pallas_call x1, Pallas kernels: 56.8 us -> 51.7 us  [local(): pl.pallas_call(kernel, out_shape=(jax.ShapeDtypeStruct((32, 4096), BF16),...]
    unnamed x4 -> x2, local copies, waits for them, and re-layouts: 2.25 us -> 1.28 us
where the time goes in v2:
time: 53.7 us; the launch traced here: 53.6 us
  Pallas kernels  51.7 us (96%)
  local copies, waits for them, and re-layouts  1.28 us (2%)
  between operations  0.64 us (1%)
    pallas_call x1, Pallas kernels, local(): pl.pallas_call(kernel, out_shape=(jax.ShapeDtypeStruct((32, 4096), BF16),...  51.7 us
    unnamed x2, local copies, waits for them, and re-layouts  1.28 us

profile of v2, /device:TPU:1, one launch (start us, length us, event | category | flops | bytes accessed | tf_op | source)
XLA Modules:
  0.0 53.6 jit_solution(12099608135960012194)
XLA Ops:
  0.6 51.7 %attention.1 = (bf16[32,4096]{1,0:T(8,128)(2,1)S(1)}, f32[4,128]{1,0:T(4,128)S(1)}) custom-call(bf16[128,1024]{1,0:T(8,128)(2,1)} %q_ref.1, bf16[128,512]{1,0:T(8,128)(2,1)} %k_ref.1, bf16[128,512]{1,0:T(8,128)(2,1)} %v_ref.1, s32[128]{0:T(128)} %order_ref.1), custom_call_target="tpu_custom_call" | custom-call | tf_op jit(solution)/shard_map/attention/pallas_call | solution.py:428
  52.3 0.7 %copy.8 = bf16[32,4096]{1,0:T(8,128)(2,1)} copy(bf16[32,4096]{1,0:T(8,128)(2,1)S(1)} %get-tuple-element.4) | data formatting | bytes 524288
  53.1 0.6 %copy.9 = f32[4,128]{1,0:T(4,128)} copy(f32[4,128]{1,0:T(4,128)S(1)} %get-tuple-element.5) | data formatting | bytes 4096

commit v3 on v2

v3 whole, which is shorter than its diff:
```python
import functools

import jax
import jax.numpy as jnp
from jax import lax
from jax.experimental import pallas as pl
from jax.experimental.pallas import tpu as pltpu
from jax.sharding import PartitionSpec as P

MESH = pl.DeviceIdType.MESH
HEAD = 256
ROWS = 128
BLK = 64
NZ, NY = 8, 4
NEG = -1e30
BIG = 1e30
SCALE = 1.4426950408889634 / 16.0
FLOOR = -1e6
LN2 = 0.6931471805599453
F32 = jnp.float32
BF16 = jnp.bfloat16

RIGHT_SLOTS = (0, 1, 2, 3, 7)
LEFT_SLOTS = (0, 4, 5, 6, 7)
SLOT_DZ = (0, -1, -2, -3, 1, 2, 3, 4)
QUERY_DY = (0, -1, 1, 2)


def combine(parts):
    top = functools.reduce(jnp.maximum, [lse for _, lse in parts])
    weights = [jnp.exp2(lse - top) for _, lse in parts]
    total = functools.reduce(jnp.add, weights)
    scale = 1.0 / total
    out = functools.reduce(jnp.add, [o.astype(F32) * (w * scale) for (o, _), w in zip(parts, weights)])
    return out, top + jnp.log2(total)


def kernel(q_ref, k_ref, v_ref, order_hbm, attn_ref, lse_ref,
           qbuf, kbuf, vbuf, vm, vsw, qpos, acc, mx, ls,
           osend, lsend, orecv, lrecv, obuf, abuf, lxs, lxr, sa, sb, pa, pb, km, qm, yard, order_ref,
           local_sem, send_sem, recv_sem):
    s = lax.axis_index("seq")
    g = lax.axis_index("head")
    z = s // (2 * NY)
    y = (s // 2) % NY
    c = s % 2

    def at(dz, dy):
        return (((z + dz + NZ) % NZ) * NY + (y + dy + NY) % NY) * 2 + c

    partner = (s + 1 - 2 * c, g)
    up, down = (at(1, 0), g), (at(-1, 0), g)
    fore, back = (at(0, 1), g), (at(0, -1), g)

    loads = [
        pltpu.make_async_copy(v_ref, vm, local_sem.at[0]),
        pltpu.make_async_copy(k_ref.at[:, pl.ds(pl.multiple_of(c * HEAD, HEAD), HEAD)], kbuf.at[0, pl.ds(0, ROWS), :], local_sem.at[1]),
    ]
    for hd in range(2):
        loads.append(pltpu.make_async_copy(
            q_ref.at[:, pl.ds(pl.multiple_of(c * 2 * HEAD + hd * HEAD, HEAD), HEAD)],
            qbuf.at[0, pl.ds(hd * ROWS, ROWS), :], local_sem.at[2 + hd]))
    loads += [
        pltpu.make_async_copy(k_ref.at[:, pl.ds(pl.multiple_of((1 - c) * HEAD, HEAD), HEAD)], km, local_sem.at[4]),
        pltpu.make_async_copy(q_ref.at[:, pl.ds(pl.multiple_of((1 - c) * 2 * HEAD, HEAD), 2 * HEAD)], qm, local_sem.at[5]),
    ]
    order_load = pltpu.make_async_copy(order_hbm, order_ref, local_sem.at[6])
    for n in (1, 4, 2, 3, 0, 5):
        loads[n].start()
    order_load.start()

    line = []
    for r in range(2):
        for e in range(4):
            if r or e:
                line.append(((s if r == 0 else s + 1 - 2 * c), (g + e) % 4))
    barrier = pltpu.get_barrier_semaphore()
    for peer in line + [up, down, fore, back]:
        pl.semaphore_signal(barrier, inc=1, device_id=peer, device_id_type=MESH)

    table = {}
    recv_slots = {}

    def recv_slot(key):
        return recv_sem.at[recv_slots.setdefault(key, len(recv_slots))]

    def message(name, src, dst, device, group, key=None):
        table[name] = pltpu.make_async_remote_copy(
            src_ref=src, dst_ref=dst, send_sem=send_sem.at[group], recv_sem=recv_slot(name if key is None else key),
            device_id=device, device_id_type=MESH)

    def drain(sem, kib):
        ref = yard.at[pl.ds(0, kib // 4)]
        pltpu.make_async_copy(ref, ref, sem).wait()

    other = 1 - c
    for hd in range(2):
        message(("xq", hd), qm.at[:, pl.ds(hd * HEAD, HEAD)], qbuf.at[4, pl.ds(hd * ROWS, ROWS), :], partner, 1)
    message("xk", km, kbuf.at[0, pl.ds(ROWS, ROWS), :], partner, 1)
    message("xv", vsw, vbuf.at[0, :, pl.ds(ROWS, ROWS)], partner, 1)
    for h in range(2):
        def kpart(slot):
            return kbuf.at[slot, pl.ds(h * ROWS, ROWS), :]

        def vpart(slot):
            return vbuf.at[slot, :, pl.ds(h * ROWS, ROWS)]

        for t in range(1, 5):
            key = ("end", h) if t == 4 else None
            message(("rk", h, t), kpart(RIGHT_SLOTS[t - 1]), kpart(RIGHT_SLOTS[t]), up, 0, key)
            message(("lv", h, t), vpart(LEFT_SLOTS[t - 1]), vpart(LEFT_SLOTS[t]), down, 0, key)
            if t < 4:
                message(("lk", h, t), kpart(LEFT_SLOTS[t - 1]), kpart(LEFT_SLOTS[t]), down, 0)
                message(("rv", h, t), vpart(RIGHT_SLOTS[t - 1]), vpart(RIGHT_SLOTS[t]), up, 0)

        def qpart(slot, hd):
            return qbuf.at[h * 4 + slot, pl.ds(hd * ROWS, ROWS), :]

        message(("qr", h, 0), qpart(0, 0), qpart(1, 0), fore, 1)
        message(("ql", h, 1), qpart(0, 1), qpart(2, 1), back, 1)
        message(("qr", h, 1), qpart(0, 1), qpart(1, 1), fore, 1, ("near", h))
        message(("ql", h, 0), qpart(0, 0), qpart(2, 0), back, 1, ("near", h))
        message(("qrr", h), qpart(1, 0), qpart(3, 0), fore, 1, ("far", h))
        message(("qll", h), qpart(2, 1), qpart(3, 1), back, 1, ("far", h))
    for n in range(6):
        device = fore if n % 2 == 0 else back
        for hd in range(2):
            message(("l", n, hd), lsend.at[2 * n + hd], lrecv.at[2 * n + hd], device, 3, ("taken", n, hd))
            message(("o", n, hd), osend.at[2 * n + hd], orecv.at[2 * n + hd], device, 2, ("taken", n, hd))
    for hd in range(2):
        message(("lx", hd), lxs.at[hd], lxr.at[hd], partner, 3, "lx")
    for r in range(2):
        for e in range(4):
            for hd in range(2):
                if r or e:
                    rows = pl.ds(pl.multiple_of(((g + e) % 4) * 32, 32), 32)
                    cols = pl.ds(pl.multiple_of(((2 * g + c) * 2 + hd) * HEAD, HEAD), HEAD)
                    there = s if r == 0 else s + 1 - 2 * c
                    message(("line", r, e, hd), obuf.at[r, rows, pl.ds(hd * HEAD, HEAD)], abuf.at[:, cols],
                            (there, (g + e) % 4), 3, "line")

    def send(name):
        table[name].start()

    def arrive(name):
        table[name].wait_recv()

    def key_bases(slot):
        out = []
        for h in range(2):
            origin = (((z + SLOT_DZ[slot] + NZ) % NZ) * NY + y) * 2 + (c if h == 0 else other)
            out += [order_ref[2 * origin] * BLK, order_ref[2 * origin + 1] * BLK]
        return out

    iota = lax.broadcasted_iota(jnp.int32, (BLK, HEAD), 0)

    score_buffers, weight_buffers = (sa, sb), (pa, pb)
    bases_of = {}
    queue = []
    count = [0]

    def stage_scores(item):
        i, slots = item["tile"], item["slots"]
        into = score_buffers[item["turn"] % 2]
        q = qbuf[i]
        for n, slot in enumerate(slots):
            into[n * 256:(n + 1) * 256, :] = lax.dot_general(
                kbuf[slot], q, (((1,), (1,)), ((), ())), preferred_element_type=F32)

    def stage_weights(item):
        i, slots = item["tile"], item["slots"]
        source, into = score_buffers[item["turn"] % 2], weight_buffers[item["turn"] % 2]
        diagonal = slots == (0,) and i in (0, 4)
        first = slots == (0,)
        position = qpos[i, 0:1, :]
        for slot in slots:
            if slot not in bases_of:
                bases_of[slot] = key_bases(slot)
        bases = [base for slot in slots for base in bases_of[slot]]

        def raw(b):
            block = source[b * BLK:(b + 1) * BLK, :]
            return jnp.where(iota <= position - bases[b], block, NEG) if diagonal else block

        old = jnp.full((1, HEAD), FLOOR, F32) if first else mx[i, 0:1, :]
        allowed = [base <= position for base in bases]
        best = functools.reduce(jnp.maximum, [
            jnp.where(allowed[b], jnp.max(raw(b).reshape(8, 8, HEAD), axis=0), NEG) for b in range(len(bases))])
        best = jnp.max(best, axis=0, keepdims=True) * SCALE
        fresh = jnp.maximum(old, best)
        sums = None
        for b in range(len(bases)):
            weights = jnp.exp2(raw(b) * SCALE - jnp.where(allowed[b], fresh, BIG))
            part = jnp.sum(weights.reshape(8, 8, HEAD), axis=0)
            sums = part if sums is None else sums + part
            into[b * BLK:(b + 1) * BLK, :] = weights.astype(BF16)
        if first:
            item["factor"] = None
        else:
            item["factor"] = jnp.exp2(old - fresh)
            sums = ls[i] * item["factor"] + sums
        if item["last"]:
            item["top"], item["sums"] = fresh, sums
        else:
            mx[i] = jnp.broadcast_to(fresh, (8, HEAD))
            ls[i] = sums

    def stage_values(item):
        i, slots = item["tile"], item["slots"]
        source = weight_buffers[item["turn"] % 2]
        update = functools.reduce(jnp.add, [
            lax.dot_general(vbuf[slot], source[n * 256:(n + 1) * 256, :], (((1,), (0,)), ((), ())), preferred_element_type=F32)
            for n, slot in enumerate(slots)
        ])
        if item["factor"] is not None:
            update = acc[i] * item["factor"] + update
        if item["last"]:
            l = jnp.sum(item["sums"], axis=0, keepdims=True)
            some = l > 0.0
            inverse = jnp.where(some, 1.0 / jnp.where(some, l, 1.0), 0.0)
            item["done"](update * inverse, jnp.where(some, item["top"] + jnp.log2(jnp.where(some, l, 1.0)), NEG))
        else:
            acc[i] = update

    def advance():
        if queue and queue[-1]["stage"] == 0:
            stage_scores(queue[-1])
        for item in queue[::-1]:
            if item["stage"] == 1:
                stage_weights(item)
            elif item["stage"] == 2:
                stage_values(item)
        for item in queue:
            item["stage"] += 1
        queue[:] = [item for item in queue if item["stage"] < 3]

    def push(tiles, slots, done=None):
        for i in tiles:
            queue.append({"tile": i, "slots": slots, "turn": count[0], "stage": 0, "last": done is not None, "done": done})
            count[0] += 1
            advance()

    def flush():
        while queue:
            advance()

    def first_hop(kind, h):
        send(("r" + kind, h, 1))
        send(("l" + kind, h, 1))

    def ring_keys(h, t):
        arrive(("rk", h, t))
        send(("rk", h, t + 1))
        arrive(("lk", h, t))
        if t < 3:
            send(("lk", h, t + 1))

    def ring_values(h, t):
        arrive(("lv", h, t))
        send(("lv", h, t + 1))
        arrive(("rv", h, t))
        if t < 3:
            send(("rv", h, t + 1))

    def ring_end(h):
        drain(recv_slot(("end", h)), 128)

    def spread(hd):
        arrive(("xq", hd))
        send(("qr", 1, hd))
        send(("ql", 1, hd))

    def relay(h):
        arrive(("qr", h, 0))
        send(("qrr", h))
        arrive(("ql", h, 1))
        send(("qll", h))
        drain(recv_slot(("near", h)), 128)

    def relayed(h):
        drain(recv_slot(("far", h)), 128)

    def cross_values():
        arrive("xv")
        first_hop("v", 1)

    def cross_keys():
        arrive("xk")
        first_hop("k", 1)

    assert len(recv_slots) == 52, len(recv_slots)
    loads[1].wait()
    loads[4].wait()
    pl.semaphore_wait(barrier, 11)
    first_hop("k", 0)
    send("xk")
    for hd in range(2):
        loads[2 + hd].wait()
        send(("qr", 0, hd))
        send(("ql", 0, hd))

    def flipped(column):
        v = vm[:, pl.ds(pl.multiple_of(column * HEAD, HEAD), HEAD)]
        return v.astype(F32).T.astype(BF16)

    loads[0].wait()
    vbuf[0, :, 0:ROWS] = flipped(c)
    vsw[...] = flipped(other)
    order_load.wait()
    lane = lax.broadcasted_iota(jnp.int32, (8, HEAD), 1)
    for slot in range(4):
        for h in range(2):
            origin = (z * NY + (y + QUERY_DY[slot] + NY) % NY) * 2 + (c if h == 0 else other)
            first, second = order_ref[2 * origin] * BLK, order_ref[2 * origin + 1] * BLK
            inside = lane % ROWS
            qpos[h * 4 + slot] = jnp.where(inside < BLK, first + inside, second + inside - BLK)
    send("xv")
    first_hop("v", 0)
    loads[5].wait()
    send(("xq", 0))
    send(("xq", 1))

    ring_keys(0, 1)
    cross_keys()
    relay(0)
    ring_values(0, 1)
    cross_values()
    push((0, 1, 2), (0,))
    spread(0)
    spread(1)
    ring_keys(0, 2)
    relayed(0)
    push((3,), (0,))
    ring_keys(1, 1)
    push((4,), (0,))
    ring_values(0, 2)
    relay(1)
    push((5, 6), (0,))
    ring_values(1, 1)
    push((0, 1, 2, 3), (1, 4))
    ring_keys(0, 3)
    push((4, 5), (1, 4))
    ring_keys(1, 2)
    ring_values(0, 3)
    push((6,), (1, 4))
    ring_values(1, 2)
    relayed(1)
    push((7,), (0,))
    push((7,), (1, 4))
    push((0, 1), (2, 5))
    ring_keys(1, 3)
    push((2, 3, 4), (2, 5))
    ring_values(1, 3)
    push((5, 6, 7), (2, 5))
    push((0, 1, 2, 3, 4, 5, 6, 7), (3, 6))
    ring_end(0)
    ring_end(1)

    def piece(i, hd):
        return acc[i, :, hd * ROWS:(hd + 1) * ROWS], mx[i, 0:1, hd * ROWS:(hd + 1) * ROWS]

    def stage_out(n, hd, o, lse):
        osend[2 * n + hd] = o.astype(BF16)
        lsend[2 * n + hd] = jnp.broadcast_to(lse, (8, ROWS))

    def ship(n, hd):
        send(("l", n, hd))
        send(("o", n, hd))

    def taken(n, hd):
        drain(recv_slot(("taken", n, hd)), 68)
        return orecv[2 * n + hd], lrecv[2 * n + hd, 0:1, :]

    direct = {3: 0, 7: 1, 6: 2, 1: 3}

    def done_with(tile):
        def done(o, lse):
            if tile in direct:
                n = direct[tile]
                for hd in range(2):
                    stage_out(n, hd, o[:, hd * ROWS:(hd + 1) * ROWS], lse[:, hd * ROWS:(hd + 1) * ROWS])
                    if n < 2 or hd == 0:
                        ship(n, hd)
            else:
                acc[tile] = o
                mx[tile] = jnp.broadcast_to(lse, (8, HEAD))
        return done

    for tile in (3, 7, 6, 1, 2, 5, 0, 4):
        push((tile,), (7,), done_with(tile))
    flush()
    for hd in range(2):
        for n, tile in ((0, 2), (1, 5)):
            stage_out(4 + n, hd, *combine([piece(tile, hd), taken(n, hd)]))
            ship(4 + n, hd)
            if hd == 0:
                ship(2 + n, 1)

    def result(r, hd):
        pieces = [piece(0, hd), taken(3, hd), taken(4, hd)] if r == 0 else [piece(4, hd), taken(2, hd), taken(5, hd)]
        out, lse = combine(pieces)
        lse = lse * LN2
        if r:
            lxs[hd] = jnp.broadcast_to(lse, (8, ROWS))
            send(("lx", hd))
        else:
            lse_ref[pl.ds(2 * c + hd, 1), :] = lse
        obuf[r, :, hd * HEAD:(hd + 1) * HEAD] = out.T.astype(BF16)
        for e in range(4):
            if r or e:
                send(("line", r, e, hd))

    for hd in range(2):
        result(0, hd)
        result(1, hd)
    cols = pl.ds(pl.multiple_of((2 * g + c) * 2 * HEAD, 2 * HEAD), 2 * HEAD)
    abuf[:, cols] = obuf[0, pl.ds(pl.multiple_of(g * 32, 32), 32), :]
    drain(recv_slot("lx"), 8)
    for hd in range(2):
        lse_ref[pl.ds(2 * other + hd, 1), :] = lxr[hd, 0:1, :]
    drain(recv_slot("line"), 224)
    attn_ref[...] = abuf[...]
    for group, kib in enumerate((28 * 64, 16 * 64, 12 * 64, 280)):
        drain(send_sem.at[group], kib)


def settle(attn_in, lse_in, attn_out, lse_out, sem):
    copies = [
        pltpu.make_async_copy(attn_in, attn_out, sem.at[0]),
        pltpu.make_async_copy(lse_in, lse_out, sem.at[1]),
    ]
    for copy in copies:
        copy.start()
    for copy in copies:
        copy.wait()


def local(queries, keys, values, block_order):
    hbm = pl.BlockSpec(memory_space=pltpu.HBM)
    vmem = pl.BlockSpec(memory_space=pltpu.VMEM)
    results = pl.pallas_call(
        kernel,
        out_shape=(
            jax.ShapeDtypeStruct((32, 4096), BF16),
            jax.ShapeDtypeStruct((4, ROWS), F32),
        ),
        in_specs=[hbm, hbm, hbm, hbm],
        out_specs=(vmem, vmem),
        scratch_shapes=[
            pltpu.VMEM((8, 256, HEAD), BF16),
            pltpu.VMEM((8, 256, HEAD), BF16),
            pltpu.VMEM((8, HEAD, 256), BF16),
            pltpu.VMEM((ROWS, 2 * HEAD), BF16),
            pltpu.VMEM((HEAD, ROWS), BF16),
            pltpu.VMEM((8, 8, HEAD), jnp.int32),
            pltpu.VMEM((8, HEAD, 256), F32),
            pltpu.VMEM((8, 8, 256), F32),
            pltpu.VMEM((8, 8, 256), F32),
            pltpu.VMEM((12, HEAD, ROWS), BF16),
            pltpu.VMEM((12, 8, ROWS), F32),
            pltpu.VMEM((12, HEAD, ROWS), BF16),
            pltpu.VMEM((12, 8, ROWS), F32),
            pltpu.VMEM((2, ROWS, 2 * HEAD), BF16),
            pltpu.VMEM((32, 4096), BF16),
            pltpu.VMEM((2, 8, ROWS), F32),
            pltpu.VMEM((2, 8, ROWS), F32),
            pltpu.VMEM((512, HEAD), F32),
            pltpu.VMEM((512, HEAD), F32),
            pltpu.VMEM((512, HEAD), BF16),
            pltpu.VMEM((512, HEAD), BF16),
            pltpu.VMEM((ROWS, HEAD), BF16),
            pltpu.VMEM((ROWS, 2 * HEAD), BF16),
            pltpu.VMEM((448, 8, ROWS), F32),
            pltpu.SMEM((128,), jnp.int32),
            pltpu.SemaphoreType.DMA((7,)),
            pltpu.SemaphoreType.DMA((4,)),
            pltpu.SemaphoreType.DMA((52,)),
        ],
        compiler_params=pltpu.CompilerParams(collective_id=0, has_side_effects=True, vmem_limit_bytes=24 * 1024 * 1024),
        name="attention",
    )(*[pltpu.with_memory_space_constraint(a, pltpu.HBM) for a in (queries, keys, values, block_order)])
    return pl.pallas_call(
        settle,
        out_shape=(
            jax.ShapeDtypeStruct((32, 4096), BF16),
            jax.ShapeDtypeStruct((4, ROWS), F32),
        ),
        in_specs=[vmem, vmem],
        out_specs=(hbm, hbm),
        scratch_shapes=[pltpu.SemaphoreType.DMA((2,))],
        compiler_params=pltpu.CompilerParams(vmem_limit_bytes=2 * 1024 * 1024),
        name="settle",
    )(*results)


def solution(mesh):
    in_specs = (P("seq", "head"), P("seq", "head"), P("seq", "head"), P())
    out_specs = (P(("seq", "head"), None), P("head", "seq"))
    return jax.shard_map(local, mesh=mesh, in_specs=in_specs, out_specs=out_specs, check_vma=False)
```

time: 53.7 us -> 50.2 us (0.935)
  Pallas kernels: 51.7 us -> 49.5 us
  local copies, waits for them, and re-layouts: 1.28 us -> 0 us
    pallas_call x1, Pallas kernels: 51.7 us -> 48.7 us  [local(): pl.pallas_call(kernel, out_shape=(jax.ShapeDtypeStruct((32, 4096), BF16),...]
    unnamed x2 -> x0, local copies, waits for them, and re-layouts: 1.28 us -> none
    pallas_call x0 -> x1, Pallas kernels: none -> 0.72 us  [local(): pl.pallas_call(settle, out_shape=(jax.ShapeDtypeStruct((32, 4096), BF16),...]
where the time goes in v3:
time: 50.2 us; the launch traced here: 50.1 us
  Pallas kernels  49.5 us (99%)
  between operations  0.64 us (1%)
    pallas_call x1, Pallas kernels, local(): pl.pallas_call(kernel, out_shape=(jax.ShapeDtypeStruct((32, 4096), BF16),...  48.7 us

profile of v3, /device:TPU:1, one launch (start us, length us, event | category | flops | bytes accessed | tf_op | source)
XLA Modules:
  0.0 50.1 jit_solution(14114212346717721615)
XLA Ops:
  0.6 48.7 %attention.1 = (bf16[32,4096]{1,0:T(8,128)(2,1)S(1)}, f32[4,128]{1,0:T(4,128)S(1)}) custom-call(bf16[128,1024]{1,0:T(8,128)(2,1)} %q_ref.1, bf16[128,512]{1,0:T(8,128)(2,1)} %k_ref.1, bf16[128,512]{1,0:T(8,128)(2,1)} %v_ref.1, s32[128]{0:T(128)} %order_hbm.1), custom_call_target="tpu_custom_call" | custom-call | tf_op jit(solution)/shard_map/attention/pallas_call | solution.py:441
  49.4 0.7 %settle.1 = (bf16[32,4096]{1,0:T(8,128)(2,1)}, f32[4,128]{1,0:T(4,128)}) custom-call(bf16[32,4096]{1,0:T(8,128)(2,1)S(1)} %get-tuple-element.4.attn_in, f32[4,128]{1,0:T(4,128)S(1)} %get-tuple-element.5.lse_in), custom_call_target="tpu_custom_call" | custom-call | tf_op jit(solution)/shard_map/settle/pallas_call | solution.py:482

commit v4 on v3

--- a/solution.py
+++ b/solution.py
@@ -250,14 +250,16 @@
 
     def ring_keys(h, t):
         arrive(("rk", h, t))
-        send(("rk", h, t + 1))
+        if (h, t) != (0, 3):
+            send(("rk", h, t + 1))
         arrive(("lk", h, t))
         if t < 3:
             send(("lk", h, t + 1))
 
     def ring_values(h, t):
         arrive(("lv", h, t))
-        send(("lv", h, t + 1))
+        if (h, t) != (0, 3):
+            send(("lv", h, t + 1))
         arrive(("rv", h, t))
         if t < 3:
             send(("rv", h, t + 1))
@@ -334,16 +336,19 @@
     ring_keys(1, 1)
     push((4,), (0,))
     ring_values(0, 2)
+    ring_values(1, 1)
+    push((0, 1), (1, 4))
     relay(1)
+    push((2, 3), (1, 4))
+    ring_keys(0, 3)
     push((5, 6), (0,))
-    ring_values(1, 1)
-    push((0, 1, 2, 3), (1, 4))
-    ring_keys(0, 3)
     push((4, 5), (1, 4))
     ring_keys(1, 2)
     ring_values(0, 3)
     push((6,), (1, 4))
     ring_values(1, 2)
+    send(("rk", 0, 4))
+    send(("lv", 0, 4))
     relayed(1)
     push((7,), (0,))
     push((7,), (1, 4))
@@ -411,8 +416,8 @@
                 send(("line", r, e, hd))
 
     for hd in range(2):
+        result(1, hd)
         result(0, hd)
-        result(1, hd)
     cols = pl.ds(pl.multiple_of((2 * g + c) * 2 * HEAD, 2 * HEAD), 2 * HEAD)
     abuf[:, cols] = obuf[0, pl.ds(pl.multiple_of(g * 32, 32), 32), :]
     drain(recv_slot("lx"), 8)

time: 50.2 us -> 48.6 us (0.968)
  Pallas kernels: 49.5 us -> 47.8 us
    pallas_call x1, Pallas kernels: 48.7 us -> 47.1 us  [local(): pl.pallas_call(kernel, out_shape=(jax.ShapeDtypeStruct((32, 4096), BF16),...]
where the time goes in v4:
time: 48.6 us; the launch traced here: 48.5 us
  Pallas kernels  47.8 us (98%)
  between operations  0.64 us (1%)
    pallas_call x1, Pallas kernels, local(): pl.pallas_call(kernel, out_shape=(jax.ShapeDtypeStruct((32, 4096), BF16),...  47.1 us

profile of v4, /device:TPU:1, one launch (start us, length us, event | category | flops | bytes accessed | tf_op | source)
XLA Modules:
  0.0 48.5 jit_solution(17771616552161901774)
XLA Ops:
  0.6 47.1 %attention.1 = (bf16[32,4096]{1,0:T(8,128)(2,1)S(1)}, f32[4,128]{1,0:T(4,128)S(1)}) custom-call(bf16[128,1024]{1,0:T(8,128)(2,1)} %q_ref.1, bf16[128,512]{1,0:T(8,128)(2,1)} %k_ref.1, bf16[128,512]{1,0:T(8,128)(2,1)} %v_ref.1, s32[128]{0:T(128)} %order_hbm.1), custom_call_target="tpu_custom_call" | custom-call | tf_op jit(solution)/shard_map/attention/pallas_call | solution.py:446
  47.8 0.7 %settle.1 = (bf16[32,4096]{1,0:T(8,128)(2,1)}, f32[4,128]{1,0:T(4,128)}) custom-call(bf16[32,4096]{1,0:T(8,128)(2,1)S(1)} %get-tuple-element.4.attn_in, f32[4,128]{1,0:T(4,128)S(1)} %get-tuple-element.5.lse_in), custom_call_target="tpu_custom_call" | custom-call | tf_op jit(solution)/shard_map/settle/pallas_call | solution.py:487

commit v5 on v4

--- a/solution.py
+++ b/solution.py
@@ -26,18 +26,14 @@
 QUERY_DY = (0, -1, 1, 2)
 
 
-def combine(parts):
-    top = functools.reduce(jnp.maximum, [lse for _, lse in parts])
-    weights = [jnp.exp2(lse - top) for _, lse in parts]
-    total = functools.reduce(jnp.add, weights)
-    scale = 1.0 / total
-    out = functools.reduce(jnp.add, [o.astype(F32) * (w * scale) for (o, _), w in zip(parts, weights)])
-    return out, top + jnp.log2(total)
+def log_total(rows):
+    top = functools.reduce(jnp.maximum, rows)
+    return top + jnp.log2(functools.reduce(jnp.add, [jnp.exp2(row - top) for row in rows]))
 
 
 def kernel(q_ref, k_ref, v_ref, order_hbm, attn_ref, lse_ref,
            qbuf, kbuf, vbuf, vm, vsw, qpos, acc, mx, ls,
-           osend, lsend, orecv, lrecv, obuf, abuf, lxs, lxr, sa, sb, pa, pb, km, qm, yard, order_ref,
+           osend, lstat, orecv, lgot, cbuf, abufc, obuf, abuf, lxs, lxr, sa, sb, pa, pb, km, qm, yard, order_ref,
            local_sem, send_sem, recv_sem):
     s = lax.axis_index("seq")
     g = lax.axis_index("head")
@@ -69,13 +65,17 @@
         loads[n].start()
     order_load.start()
 
-    line = []
-    for r in range(2):
-        for e in range(4):
-            if r or e:
-                line.append(((s if r == 0 else s + 1 - 2 * c), (g + e) % 4))
+    def across(index):
+        return index + 1 - 2 * c
+
+    far = (at(0, 2), g)
+    peers = [up, down, fore, back]
+    for e in range(4):
+        peers.append((across(s), (g + e) % 4))
+        if e:
+            peers.append((s, (g + e) % 4))
     barrier = pltpu.get_barrier_semaphore()
-    for peer in line + [up, down, fore, back]:
+    for peer in peers:
         pl.semaphore_signal(barrier, inc=1, device_id=peer, device_id_type=MESH)
 
     table = {}
@@ -122,22 +122,24 @@
         message(("ql", h, 0), qpart(0, 0), qpart(2, 0), back, 1, ("near", h))
         message(("qrr", h), qpart(1, 0), qpart(3, 0), fore, 1, ("far", h))
         message(("qll", h), qpart(2, 1), qpart(3, 1), back, 1, ("far", h))
-    for n in range(6):
-        device = fore if n % 2 == 0 else back
+    for n in range(4):
         for hd in range(2):
-            message(("l", n, hd), lsend.at[2 * n + hd], lrecv.at[2 * n + hd], device, 3, ("taken", n, hd))
-            message(("o", n, hd), osend.at[2 * n + hd], orecv.at[2 * n + hd], device, 2, ("taken", n, hd))
+            message(("o", n, hd), osend.at[2 * n + hd], orecv.at[2 * n + hd], fore if n % 2 == 0 else back, 2)
+    for n, device in enumerate((fore, back, far)):
+        message(("stat", n), lstat, lgot.at[n], device, 3, "stat")
     for hd in range(2):
         message(("lx", hd), lxs.at[hd], lxr.at[hd], partner, 3, "lx")
-    for r in range(2):
+    for hd in range(2):
+        cols = pl.ds(pl.multiple_of(((2 * g + c) * 2 + hd) * HEAD, HEAD), HEAD)
+        half_cols = pl.ds(hd * HEAD, HEAD)
         for e in range(4):
-            for hd in range(2):
+            there = (g + e) % 4
+            rows = pl.ds(pl.multiple_of(there * 32, 32), 32)
+            for n, target in enumerate((at(0, 1), across(at(0, -1)))):
+                message(("side", n, e, hd), cbuf.at[n, rows, half_cols], abufc.at[:, cols], (target, there), 2, "side")
+            for r, target in enumerate((s, across(s))):
                 if r or e:
-                    rows = pl.ds(pl.multiple_of(((g + e) % 4) * 32, 32), 32)
-                    cols = pl.ds(pl.multiple_of(((2 * g + c) * 2 + hd) * HEAD, HEAD), HEAD)
-                    there = s if r == 0 else s + 1 - 2 * c
-                    message(("line", r, e, hd), obuf.at[r, rows, pl.ds(hd * HEAD, HEAD)], abuf.at[:, cols],
-                            (there, (g + e) % 4), 3, "line")
+                    message(("line", r, e, hd), obuf.at[r, rows, half_cols], abuf.at[:, cols], (target, there), 3, "line")
 
     def send(name):
         table[name].start()
@@ -290,10 +292,10 @@
         arrive("xk")
         first_hop("k", 1)
 
-    assert len(recv_slots) == 52, len(recv_slots)
+    assert len(recv_slots) == 50, len(recv_slots)
     loads[1].wait()
     loads[4].wait()
-    pl.semaphore_wait(barrier, 11)
+    pl.semaphore_wait(barrier, len(peers))
     first_hop("k", 0)
     send("xk")
     for hd in range(2):
@@ -361,71 +363,76 @@
     ring_end(0)
     ring_end(1)
 
-    def piece(i, hd):
-        return acc[i, :, hd * ROWS:(hd + 1) * ROWS], mx[i, 0:1, hd * ROWS:(hd + 1) * ROWS]
-
-    def stage_out(n, hd, o, lse):
-        osend[2 * n + hd] = o.astype(BF16)
-        lsend[2 * n + hd] = jnp.broadcast_to(lse, (8, ROWS))
-
-    def ship(n, hd):
-        send(("l", n, hd))
-        send(("o", n, hd))
-
-    def taken(n, hd):
-        drain(recv_slot(("taken", n, hd)), 68)
-        return orecv[2 * n + hd], lrecv[2 * n + hd, 0:1, :]
+    def half(hd):
+        return slice(hd * ROWS, (hd + 1) * ROWS)
 
     direct = {3: 0, 7: 1, 6: 2, 1: 3}
 
     def done_with(tile):
         def done(o, lse):
+            lstat[tile:tile + 1, :] = lse
             if tile in direct:
                 n = direct[tile]
                 for hd in range(2):
-                    stage_out(n, hd, o[:, hd * ROWS:(hd + 1) * ROWS], lse[:, hd * ROWS:(hd + 1) * ROWS])
-                    if n < 2 or hd == 0:
-                        ship(n, hd)
+                    osend[2 * n + hd] = o[:, half(hd)].astype(BF16)
+                    if n < 2 and hd == 0:
+                        send(("o", n, hd))
             else:
                 acc[tile] = o
-                mx[tile] = jnp.broadcast_to(lse, (8, HEAD))
         return done
 
     for tile in (3, 7, 6, 1, 2, 5, 0, 4):
         push((tile,), (7,), done_with(tile))
     flush()
-    for hd in range(2):
-        for n, tile in ((0, 2), (1, 5)):
-            stage_out(4 + n, hd, *combine([piece(tile, hd), taken(n, hd)]))
-            ship(4 + n, hd)
-            if hd == 0:
-                ship(2 + n, 1)
-
-    def result(r, hd):
-        pieces = [piece(0, hd), taken(3, hd), taken(4, hd)] if r == 0 else [piece(4, hd), taken(2, hd), taken(5, hd)]
-        out, lse = combine(pieces)
-        lse = lse * LN2
-        if r:
-            lxs[hd] = jnp.broadcast_to(lse, (8, ROWS))
-            send(("lx", hd))
-        else:
-            lse_ref[pl.ds(2 * c + hd, 1), :] = lse
-        obuf[r, :, hd * HEAD:(hd + 1) * HEAD] = out.T.astype(BF16)
-        for e in range(4):
-            if r or e:
-                send(("line", r, e, hd))
-
-    for hd in range(2):
-        result(1, hd)
-        result(0, hd)
+    for n in range(3):
+        send(("stat", n))
+    for n, hd in ((0, 1), (1, 1), (2, 0), (3, 0), (2, 1), (3, 1)):
+        send(("o", n, hd))
+    drain(recv_slot("stat"), 24)
+
+    def mine(i):
+        return lstat[i:i + 1, :]
+
+    def theirs(n, i):
+        return lgot[n, i:i + 1, :]
+
+    side_total = [
+        log_total([mine(2), theirs(0, 3), theirs(1, 0), theirs(2, 1)]),
+        log_total([mine(5), theirs(1, 7), theirs(0, 4), theirs(2, 6)]),
+    ]
+    own_total = [log_total([mine(4 * h), theirs(0, 4 * h + 2), theirs(1, 4 * h + 1), theirs(2, 4 * h + 3)]) for h in range(2)]
+    for hd in range(2):
+        lxs[hd] = jnp.broadcast_to(own_total[1][:, half(hd)] * LN2, (8, ROWS))
+        send(("lx", hd))
+        lse_ref[pl.ds(2 * c + hd, 1), :] = own_total[0][:, half(hd)] * LN2
+
+    def joined(tile, n, hd, total, lse):
+        arrive(("o", n, hd))
+        out = acc[tile, :, half(hd)] * jnp.exp2(mine(tile) - total)[:, half(hd)]
+        out = out + orecv[2 * n + hd].astype(F32) * jnp.exp2(lse - total)[:, half(hd)]
+        return out.T.astype(BF16)
+
+    for hd in range(2):
+        for n, tile, lse in ((0, 2, theirs(0, 3)), (1, 5, theirs(1, 7))):
+            cbuf[n, :, hd * HEAD:(hd + 1) * HEAD] = joined(tile, n, hd, side_total[n], lse)
+            for e in (1, 2, 3, 0):
+                send(("side", n, e, hd))
+    for hd in range(2):
+        for r, n, lse in ((1, 2, theirs(0, 6)), (0, 3, theirs(1, 1))):
+            obuf[r, :, hd * HEAD:(hd + 1) * HEAD] = joined(4 * r, n, hd, own_total[r], lse)
+            for e in range(4):
+                if r or e:
+                    send(("line", r, e, hd))
+
     cols = pl.ds(pl.multiple_of((2 * g + c) * 2 * HEAD, 2 * HEAD), 2 * HEAD)
     abuf[:, cols] = obuf[0, pl.ds(pl.multiple_of(g * 32, 32), 32), :]
     drain(recv_slot("lx"), 8)
     for hd in range(2):
         lse_ref[pl.ds(2 * other + hd, 1), :] = lxr[hd, 0:1, :]
     drain(recv_slot("line"), 224)
-    attn_ref[...] = abuf[...]
-    for group, kib in enumerate((28 * 64, 16 * 64, 12 * 64, 280)):
+    drain(recv_slot("side"), 256)
+    attn_ref[...] = (abuf[...].astype(F32) + abufc[...].astype(F32)).astype(BF16)
+    for group, kib in enumerate((28 * 64, 16 * 64, 8 * 64 + 256, 256)):
         drain(send_sem.at[group], kib)
 
 
@@ -461,10 +468,12 @@
             pltpu.VMEM((8, HEAD, 256), F32),
             pltpu.VMEM((8, 8, 256), F32),
             pltpu.VMEM((8, 8, 256), F32),
-            pltpu.VMEM((12, HEAD, ROWS), BF16),
-            pltpu.VMEM((12, 8, ROWS), F32),
-            pltpu.VMEM((12, HEAD, ROWS), BF16),
-            pltpu.VMEM((12, 8, ROWS), F32),
+            pltpu.VMEM((8, HEAD, ROWS), BF16),
+            pltpu.VMEM((8, HEAD), F32),
+            pltpu.VMEM((8, HEAD, ROWS), BF16),
+            pltpu.VMEM((3, 8, HEAD), F32),
+            pltpu.VMEM((2, ROWS, 2 * HEAD), BF16),
+            pltpu.VMEM((32, 4096), BF16),
             pltpu.VMEM((2, ROWS, 2 * HEAD), BF16),
             pltpu.VMEM((32, 4096), BF16),
             pltpu.VMEM((2, 8, ROWS), F32),
@@ -479,7 +488,7 @@
             pltpu.SMEM((128,), jnp.int32),
             pltpu.SemaphoreType.DMA((7,)),
             pltpu.SemaphoreType.DMA((4,)),
-            pltpu.SemaphoreType.DMA((52,)),
+            pltpu.SemaphoreType.DMA((50,)),
         ],
         compiler_params=pltpu.CompilerParams(collective_id=0, has_side_effects=True, vmem_limit_bytes=24 * 1024 * 1024),
         name="attention",

time: 48.6 us -> 47.8 us (0.984)
  Pallas kernels: 47.8 us -> 47.1 us
    pallas_call x1, Pallas kernels: 47.1 us -> 46.4 us  [local(): pl.pallas_call(kernel, out_shape=(jax.ShapeDtypeStruct((32, 4096), BF16),...]
where the time goes in v5:
time: 47.8 us; the launch traced here: 47.7 us
  Pallas kernels  47.1 us (99%)
  between operations  0.64 us (1%)
    pallas_call x1, Pallas kernels, local(): pl.pallas_call(kernel, out_shape=(jax.ShapeDtypeStruct((32, 4096), BF16),...  46.4 us

profile of v5, /device:TPU:1, one launch (start us, length us, event | category | flops | bytes accessed | tf_op | source)
XLA Modules:
  0.0 47.7 jit_solution(15616828384900148621)
XLA Ops:
  0.6 46.4 %attention.1 = (bf16[32,4096]{1,0:T(8,128)(2,1)S(1)}, f32[4,128]{1,0:T(4,128)S(1)}) custom-call(bf16[128,1024]{1,0:T(8,128)(2,1)} %q_ref.1, bf16[128,512]{1,0:T(8,128)(2,1)} %k_ref.1, bf16[128,512]{1,0:T(8,128)(2,1)} %v_ref.1, s32[128]{0:T(128)} %order_hbm.1), custom_call_target="tpu_custom_call" | custom-call | tf_op jit(solution)/shard_map/attention/pallas_call | solution.py:453
  47.0 0.7 %settle.1 = (bf16[32,4096]{1,0:T(8,128)(2,1)}, f32[4,128]{1,0:T(4,128)}) custom-call(bf16[32,4096]{1,0:T(8,128)(2,1)S(1)} %get-tuple-element.4.attn_in, f32[4,128]{1,0:T(4,128)S(1)} %get-tuple-element.5.lse_in), custom_call_target="tpu_custom_call" | custom-call | tf_op jit(solution)/shard_map/settle/pallas_call | solution.py:496

commit v6 on v5

--- a/solution.py
+++ b/solution.py
@@ -61,22 +61,24 @@
         pltpu.make_async_copy(q_ref.at[:, pl.ds(pl.multiple_of((1 - c) * 2 * HEAD, HEAD), 2 * HEAD)], qm, local_sem.at[5]),
     ]
     order_load = pltpu.make_async_copy(order_hbm, order_ref, local_sem.at[6])
-    for n in (1, 4, 2, 3, 0, 5):
-        loads[n].start()
-    order_load.start()
+    loads[1].start()
 
     def across(index):
         return index + 1 - 2 * c
 
     far = (at(0, 2), g)
+    members = (g, g + 1 - 2 * (g % 2), (g + 2) % 4, 3 - g)
     peers = [up, down, fore, back]
     for e in range(4):
-        peers.append((across(s), (g + e) % 4))
+        peers.append((across(s), members[e]))
         if e:
-            peers.append((s, (g + e) % 4))
+            peers.append((s, members[e]))
     barrier = pltpu.get_barrier_semaphore()
     for peer in peers:
         pl.semaphore_signal(barrier, inc=1, device_id=peer, device_id_type=MESH)
+    for n in (4, 2, 3, 0, 5):
+        loads[n].start()
+    order_load.start()
 
     table = {}
     recv_slots = {}
@@ -99,19 +101,21 @@
     message("xk", km, kbuf.at[0, pl.ds(ROWS, ROWS), :], partner, 1)
     message("xv", vsw, vbuf.at[0, :, pl.ds(ROWS, ROWS)], partner, 1)
     for h in range(2):
-        def kpart(slot):
-            return kbuf.at[slot, pl.ds(h * ROWS, ROWS), :]
-
-        def vpart(slot):
-            return vbuf.at[slot, :, pl.ds(h * ROWS, ROWS)]
-
-        for t in range(1, 5):
-            key = ("end", h) if t == 4 else None
-            message(("rk", h, t), kpart(RIGHT_SLOTS[t - 1]), kpart(RIGHT_SLOTS[t]), up, 0, key)
-            message(("lv", h, t), vpart(LEFT_SLOTS[t - 1]), vpart(LEFT_SLOTS[t]), down, 0, key)
-            if t < 4:
-                message(("lk", h, t), kpart(LEFT_SLOTS[t - 1]), kpart(LEFT_SLOTS[t]), down, 0)
-                message(("rv", h, t), vpart(RIGHT_SLOTS[t - 1]), vpart(RIGHT_SLOTS[t]), up, 0)
+        for p in range(2):
+            def kpart(slot):
+                return kbuf.at[slot, pl.ds(h * ROWS + p * BLK, BLK), :]
+
+            def vpart(slot):
+                return vbuf.at[slot, pl.ds(p * ROWS, ROWS), pl.ds(h * ROWS, ROWS)]
+
+            for t in range(1, 5):
+                key = ("end", h) if t == 4 else None
+                message(("rk", h, t, p), kpart(RIGHT_SLOTS[t - 1]), kpart(RIGHT_SLOTS[t]), up, 0, key)
+                message(("lv", h, t, p), vpart(LEFT_SLOTS[t - 1]), vpart(LEFT_SLOTS[t]), down, 0, key)
+                if t < 4:
+                    key_k, key_v = (("third_k", h), ("third_v", h)) if t == 3 else (None, None)
+                    message(("lk", h, t, p), kpart(LEFT_SLOTS[t - 1]), kpart(LEFT_SLOTS[t]), down, 0, key_k)
+                    message(("rv", h, t, p), vpart(RIGHT_SLOTS[t - 1]), vpart(RIGHT_SLOTS[t]), up, 0, key_v)
 
         def qpart(slot, hd):
             return qbuf.at[h * 4 + slot, pl.ds(hd * ROWS, ROWS), :]
@@ -133,7 +137,7 @@
         cols = pl.ds(pl.multiple_of(((2 * g + c) * 2 + hd) * HEAD, HEAD), HEAD)
         half_cols = pl.ds(hd * HEAD, HEAD)
         for e in range(4):
-            there = (g + e) % 4
+            there = members[e]
             rows = pl.ds(pl.multiple_of(there * 32, 32), 32)
             for n, target in enumerate((at(0, 1), across(at(0, -1)))):
                 message(("side", n, e, hd), cbuf.at[n, rows, half_cols], abufc.at[:, cols], (target, there), 2, "side")
@@ -247,24 +251,35 @@
             advance()
 
     def first_hop(kind, h):
-        send(("r" + kind, h, 1))
-        send(("l" + kind, h, 1))
+        for p in range(2):
+            send(("r" + kind, h, 1, p))
+            send(("l" + kind, h, 1, p))
+
+    def last_hop(h, p):
+        send(("rk", h, 4, p))
+        send(("lv", h, 4, p))
 
     def ring_keys(h, t):
-        arrive(("rk", h, t))
-        if (h, t) != (0, 3):
-            send(("rk", h, t + 1))
-        arrive(("lk", h, t))
-        if t < 3:
-            send(("lk", h, t + 1))
+        for p in range(2):
+            arrive(("rk", h, t, p))
+            if (h, t) != (0, 3):
+                send(("rk", h, t + 1, p))
+            if t < 3:
+                arrive(("lk", h, t, p))
+                send(("lk", h, t + 1, p))
+        if t == 3:
+            drain(recv_slot(("third_k", h)), 64)
 
     def ring_values(h, t):
-        arrive(("lv", h, t))
-        if (h, t) != (0, 3):
-            send(("lv", h, t + 1))
-        arrive(("rv", h, t))
-        if t < 3:
-            send(("rv", h, t + 1))
+        for p in range(2):
+            arrive(("lv", h, t, p))
+            if (h, t) != (0, 3):
+                send(("lv", h, t + 1, p))
+            if t < 3:
+                arrive(("rv", h, t, p))
+                send(("rv", h, t + 1, p))
+        if t == 3:
+            drain(recv_slot(("third_v", h)), 64)
 
     def ring_end(h):
         drain(recv_slot(("end", h)), 128)
@@ -292,7 +307,7 @@
         arrive("xk")
         first_hop("k", 1)
 
-    assert len(recv_slots) == 50, len(recv_slots)
+    assert len(recv_slots) == 70, len(recv_slots)
     loads[1].wait()
     loads[4].wait()
     pl.semaphore_wait(barrier, len(peers))
@@ -349,8 +364,8 @@
     ring_values(0, 3)
     push((6,), (1, 4))
     ring_values(1, 2)
-    send(("rk", 0, 4))
-    send(("lv", 0, 4))
+    for p in range(2):
+        last_hop(0, p)
     relayed(1)
     push((7,), (0,))
     push((7,), (1, 4))
@@ -415,14 +430,13 @@
     for hd in range(2):
         for n, tile, lse in ((0, 2, theirs(0, 3)), (1, 5, theirs(1, 7))):
             cbuf[n, :, hd * HEAD:(hd + 1) * HEAD] = joined(tile, n, hd, side_total[n], lse)
-            for e in (1, 2, 3, 0):
+            for e in (2, 3, 1, 0) if n == 0 else (0, 1, 2, 3):
                 send(("side", n, e, hd))
     for hd in range(2):
         for r, n, lse in ((1, 2, theirs(0, 6)), (0, 3, theirs(1, 1))):
             obuf[r, :, hd * HEAD:(hd + 1) * HEAD] = joined(4 * r, n, hd, own_total[r], lse)
-            for e in range(4):
-                if r or e:
-                    send(("line", r, e, hd))
+            for e in (0, 1, 2, 3) if r else (2, 3, 1):
+                send(("line", r, e, hd))
 
     cols = pl.ds(pl.multiple_of((2 * g + c) * 2 * HEAD, 2 * HEAD), 2 * HEAD)
     abuf[:, cols] = obuf[0, pl.ds(pl.multiple_of(g * 32, 32), 32), :]
@@ -488,7 +502,7 @@
             pltpu.SMEM((128,), jnp.int32),
             pltpu.SemaphoreType.DMA((7,)),
             pltpu.SemaphoreType.DMA((4,)),
-            pltpu.SemaphoreType.DMA((50,)),
+            pltpu.SemaphoreType.DMA((70,)),
         ],
         compiler_params=pltpu.CompilerParams(collective_id=0, has_side_effects=True, vmem_limit_bytes=24 * 1024 * 1024),
         name="attention",

time: 47.8 us -> 47.3 us (0.990)
  Pallas kernels: 47.1 us -> 46.6 us
    pallas_call x1, Pallas kernels: 46.4 us -> 45.8 us  [local(): pl.pallas_call(kernel, out_shape=(jax.ShapeDtypeStruct((32, 4096), BF16),...]
where the time goes in v6:
time: 47.3 us; the launch traced here: 47.2 us
  Pallas kernels  46.6 us (99%)
  between operations  0.64 us (1%)
    pallas_call x1, Pallas kernels, local(): pl.pallas_call(kernel, out_shape=(jax.ShapeDtypeStruct((32, 4096), BF16),...  45.8 us

profile of v6, /device:TPU:1, one launch (start us, length us, event | category | flops | bytes accessed | tf_op | source)
XLA Modules:
  0.0 47.2 jit_solution(7705566724983084881)
XLA Ops:
  0.6 45.8 %attention.1 = (bf16[32,4096]{1,0:T(8,128)(2,1)S(1)}, f32[4,128]{1,0:T(4,128)S(1)}) custom-call(bf16[128,1024]{1,0:T(8,128)(2,1)} %q_ref.1, bf16[128,512]{1,0:T(8,128)(2,1)} %k_ref.1, bf16[128,512]{1,0:T(8,128)(2,1)} %v_ref.1, s32[128]{0:T(128)} %order_hbm.1), custom_call_target="tpu_custom_call" | custom-call | tf_op jit(solution)/shard_map/attention/pallas_call | solution.py:467
  46.5 0.7 %settle.1 = (bf16[32,4096]{1,0:T(8,128)(2,1)}, f32[4,128]{1,0:T(4,128)}) custom-call(bf16[32,4096]{1,0:T(8,128)(2,1)S(1)} %get-tuple-element.4.attn_in, f32[4,128]{1,0:T(4,128)S(1)} %get-tuple-element.5.lse_in), custom_call_target="tpu_custom_call" | custom-call | tf_op jit(solution)/shard_map/settle/pallas_call | solution.py:510

commit v7 on v6

--- a/solution.py
+++ b/solution.py
@@ -109,26 +109,25 @@
                 return vbuf.at[slot, pl.ds(p * ROWS, ROWS), pl.ds(h * ROWS, ROWS)]
 
             for t in range(1, 5):
-                key = ("end", h) if t == 4 else None
-                message(("rk", h, t, p), kpart(RIGHT_SLOTS[t - 1]), kpart(RIGHT_SLOTS[t]), up, 0, key)
-                message(("lv", h, t, p), vpart(LEFT_SLOTS[t - 1]), vpart(LEFT_SLOTS[t]), down, 0, key)
+                key_k, key_v = (("end", h), ("end", h)) if t == 4 else (("k", h, t, p), ("v", h, t, p))
+                message(("rk", h, t, p), kpart(RIGHT_SLOTS[t - 1]), kpart(RIGHT_SLOTS[t]), up, 0, key_k)
+                message(("lv", h, t, p), vpart(LEFT_SLOTS[t - 1]), vpart(LEFT_SLOTS[t]), down, 0, key_v)
                 if t < 4:
-                    key_k, key_v = (("third_k", h), ("third_v", h)) if t == 3 else (None, None)
                     message(("lk", h, t, p), kpart(LEFT_SLOTS[t - 1]), kpart(LEFT_SLOTS[t]), down, 0, key_k)
                     message(("rv", h, t, p), vpart(RIGHT_SLOTS[t - 1]), vpart(RIGHT_SLOTS[t]), up, 0, key_v)
 
         def qpart(slot, hd):
             return qbuf.at[h * 4 + slot, pl.ds(hd * ROWS, ROWS), :]
 
-        message(("qr", h, 0), qpart(0, 0), qpart(1, 0), fore, 1)
-        message(("ql", h, 1), qpart(0, 1), qpart(2, 1), back, 1)
+        message(("qr", h, 0), qpart(0, 0), qpart(1, 0), fore, 1, ("pass", h))
+        message(("ql", h, 1), qpart(0, 1), qpart(2, 1), back, 1, ("pass", h))
         message(("qr", h, 1), qpart(0, 1), qpart(1, 1), fore, 1, ("near", h))
         message(("ql", h, 0), qpart(0, 0), qpart(2, 0), back, 1, ("near", h))
         message(("qrr", h), qpart(1, 0), qpart(3, 0), fore, 1, ("far", h))
         message(("qll", h), qpart(2, 1), qpart(3, 1), back, 1, ("far", h))
     for n in range(4):
         for hd in range(2):
-            message(("o", n, hd), osend.at[2 * n + hd], orecv.at[2 * n + hd], fore if n % 2 == 0 else back, 2)
+            message(("o", n, hd), osend.at[2 * n + hd], orecv.at[2 * n + hd], fore if n % 2 == 0 else back, 2, ("o", n // 2, hd))
     for n, device in enumerate((fore, back, far)):
         message(("stat", n), lstat, lgot.at[n], device, 3, "stat")
     for hd in range(2):
@@ -261,25 +260,19 @@
 
     def ring_keys(h, t):
         for p in range(2):
-            arrive(("rk", h, t, p))
+            drain(recv_slot(("k", h, t, p)), 64)
             if (h, t) != (0, 3):
                 send(("rk", h, t + 1, p))
             if t < 3:
-                arrive(("lk", h, t, p))
                 send(("lk", h, t + 1, p))
-        if t == 3:
-            drain(recv_slot(("third_k", h)), 64)
 
     def ring_values(h, t):
         for p in range(2):
-            arrive(("lv", h, t, p))
+            drain(recv_slot(("v", h, t, p)), 64)
             if (h, t) != (0, 3):
                 send(("lv", h, t + 1, p))
             if t < 3:
-                arrive(("rv", h, t, p))
                 send(("rv", h, t + 1, p))
-        if t == 3:
-            drain(recv_slot(("third_v", h)), 64)
 
     def ring_end(h):
         drain(recv_slot(("end", h)), 128)
@@ -290,9 +283,8 @@
         send(("ql", 1, hd))
 
     def relay(h):
-        arrive(("qr", h, 0))
+        drain(recv_slot(("pass", h)), 128)
         send(("qrr", h))
-        arrive(("ql", h, 1))
         send(("qll", h))
         drain(recv_slot(("near", h)), 128)
 
@@ -307,7 +299,7 @@
         arrive("xk")
         first_hop("k", 1)
 
-    assert len(recv_slots) == 70, len(recv_slots)
+    assert len(recv_slots) == 44, len(recv_slots)
     loads[1].wait()
     loads[4].wait()
     pl.semaphore_wait(barrier, len(peers))
@@ -347,10 +339,10 @@
     push((0, 1, 2), (0,))
     spread(0)
     spread(1)
+    ring_keys(1, 1)
     ring_keys(0, 2)
     relayed(0)
     push((3,), (0,))
-    ring_keys(1, 1)
     push((4,), (0,))
     ring_values(0, 2)
     ring_values(1, 1)
@@ -422,17 +414,18 @@
         lse_ref[pl.ds(2 * c + hd, 1), :] = own_total[0][:, half(hd)] * LN2
 
     def joined(tile, n, hd, total, lse):
-        arrive(("o", n, hd))
         out = acc[tile, :, half(hd)] * jnp.exp2(mine(tile) - total)[:, half(hd)]
         out = out + orecv[2 * n + hd].astype(F32) * jnp.exp2(lse - total)[:, half(hd)]
         return out.T.astype(BF16)
 
     for hd in range(2):
+        drain(recv_slot(("o", 0, hd)), 128)
         for n, tile, lse in ((0, 2, theirs(0, 3)), (1, 5, theirs(1, 7))):
             cbuf[n, :, hd * HEAD:(hd + 1) * HEAD] = joined(tile, n, hd, side_total[n], lse)
             for e in (2, 3, 1, 0) if n == 0 else (0, 1, 2, 3):
                 send(("side", n, e, hd))
     for hd in range(2):
+        drain(recv_slot(("o", 1, hd)), 128)
         for r, n, lse in ((1, 2, theirs(0, 6)), (0, 3, theirs(1, 1))):
             obuf[r, :, hd * HEAD:(hd + 1) * HEAD] = joined(4 * r, n, hd, own_total[r], lse)
             for e in (0, 1, 2, 3) if r else (2, 3, 1):
@@ -502,7 +495,7 @@
             pltpu.SMEM((128,), jnp.int32),
             pltpu.SemaphoreType.DMA((7,)),
             pltpu.SemaphoreType.DMA((4,)),
-            pltpu.SemaphoreType.DMA((70,)),
+            pltpu.SemaphoreType.DMA((44,)),
         ],
         compiler_params=pltpu.CompilerParams(collective_id=0, has_side_effects=True, vmem_limit_bytes=24 * 1024 * 1024),
         name="attention",

time: 47.3 us -> 47.4 us (level)
  no operation moved by 1% of the time
where the time goes in v7:
time: 47.4 us; the launch traced here: 47.3 us
  Pallas kernels  46.6 us (98%)
  between operations  0.64 us (1%)
    pallas_call x1, Pallas kernels, local(): pl.pallas_call(kernel, out_shape=(jax.ShapeDtypeStruct((32, 4096), BF16),...  45.9 us

profile of v7, /device:TPU:1, one launch (start us, length us, event | category | flops | bytes accessed | tf_op | source)
XLA Modules:
  0.0 47.3 jit_solution(2846199069224800075)
XLA Ops:
  0.6 45.9 %attention.1 = (bf16[32,4096]{1,0:T(8,128)(2,1)S(1)}, f32[4,128]{1,0:T(4,128)S(1)}) custom-call(bf16[128,1024]{1,0:T(8,128)(2,1)} %q_ref.1, bf16[128,512]{1,0:T(8,128)(2,1)} %k_ref.1, bf16[128,512]{1,0:T(8,128)(2,1)} %v_ref.1, s32[128]{0:T(128)} %order_hbm.1), custom_call_target="tpu_custom_call" | custom-call | tf_op jit(solution)/shard_map/attention/pallas_call | solution.py:460
  46.5 0.7 %settle.1 = (bf16[32,4096]{1,0:T(8,128)(2,1)}, f32[4,128]{1,0:T(4,128)}) custom-call(bf16[32,4096]{1,0:T(8,128)(2,1)S(1)} %get-tuple-element.4.attn_in, f32[4,128]{1,0:T(4,128)S(1)} %get-tuple-element.5.lse_in), custom_call_target="tpu_custom_call" | custom-call | tf_op jit(solution)/shard_map/settle/pallas_call | solution.py:503
